TPU v7x, 8 devices: a whole 2x2x1 slice. The times are simulated.
8 devices in a mesh: rep: 1 (over z), tp: 2 (over y), sp: 4 (over x, core).
Axes of the slice: x: 2, y: 2, z: 1, core: 2. Of those that a mesh axis runs over, the one named last changes fastest.
Arguments:
- x: bfloat16 [4096, 4096], P(('rep', 'sp'))
- pos: int32 [4096], P(('rep', 'sp'))
- g1: float32 [4096], replicated
- g2: float32 [4096], replicated
- wq: bfloat16 [4096, 4096], P(None, 'tp')
- wk: bfloat16 [4096, 1024], P(None, 'tp')
- wv: bfloat16 [4096, 1024], P(None, 'tp')
- wo: bfloat16 [4096, 4096], P('tp')
- w1: bfloat16 [4096, 14336], P(None, 'tp')
- w3: bfloat16 [4096, 14336], P(None, 'tp')
- w2: bfloat16 [14336, 4096], P('tp')
Outputs:
- output 1: bfloat16 [4096, 4096], P(('rep', 'sp'))
- output 2: bfloat16 [4096, 8, 128], P('rep', ('tp', 'sp'))
- output 3: bfloat16 [4096, 8, 128], P('rep', ('tp', 'sp'))
All inputs are finite; a program needn't handle non-finite values.
Results may differ from a plain program's by a relative error of at most 0.00750525.
Values are sent between devices in bfloat16 or wider.
A program may use at most 1 GiB of HBM per device.

v0:
```python
import jax
import jax.numpy as jnp
from jax import lax
from jax.sharding import PartitionSpec as P

HEAD_DIM = 128
EPS = 1e-5
ROPE_BASE = 5e5
QBLOCK = 512
NEG = -1e30


def _rms(x, g):
    x32 = x.astype(jnp.float32)
    r = lax.rsqrt(jnp.mean(x32 * x32, axis=-1, keepdims=True) + EPS)
    return (x32 * r * g).astype(jnp.bfloat16)


def _angles(pos):
    half = HEAD_DIM // 2
    inv = ROPE_BASE ** (-2.0 * jnp.arange(half, dtype=jnp.float32) / HEAD_DIM)
    ang = pos.astype(jnp.float32)[..., None] * inv
    return jnp.cos(ang)[..., None, :], jnp.sin(ang)[..., None, :]


def _rope(t, cs):
    c, s = cs
    half = HEAD_DIM // 2
    t1, t2 = t[..., :half], t[..., half:]
    return jnp.concatenate([t1 * c - t2 * s, t2 * c + t1 * s], axis=-1)


def _attention(q, k, v, row0):
    n, nk = q.shape[0], k.shape[0]
    bq = min(QBLOCK, n)
    scale = HEAD_DIM ** -0.5
    kh = k.transpose(1, 0, 2)
    vh = v.transpose(1, 0, 2)
    out = []
    for i in range(n // bq):
        lo = row0 + i * bq
        hi = min(lo + bq, nk)
        s = jnp.einsum("qkgd,knd->kgqn", q[i * bq:(i + 1) * bq], kh[:, :hi], preferred_element_type=jnp.float32) * scale
        rows = lo + jnp.arange(bq)
        s = jnp.where(rows[:, None] >= jnp.arange(hi)[None, :], s, NEG)
        p = jax.nn.softmax(s, axis=-1).astype(jnp.bfloat16)
        out.append(jnp.einsum("kgqn,knd->qkgd", p, vh[:, :hi], preferred_element_type=jnp.float32).astype(jnp.bfloat16))
    return jnp.concatenate(out, axis=0).reshape(n, -1)


def solution(mesh):
    sp = mesh.shape["sp"]
    tok = P(("rep", "sp"), None)
    col = P(None, "tp")
    row = P("tp", None)
    cache = P("rep", ("tp", "sp"), None)

    def local(x, pos, g1, g2, wq, wk, wv, wo, w1, w3, w2):
        m = x.shape[0]
        n = m * sp
        ht = wq.shape[1] // HEAD_DIM
        kt = wk.shape[1] // HEAD_DIM
        qh = ht // sp
        kd = max(1, kt // sp)
        r = sp * kd // kt
        u = _rms(x, g1)
        cs = _angles(pos)
        q = _rope(jnp.dot(u, wq, preferred_element_type=jnp.float32).reshape(m, ht, HEAD_DIM), cs).astype(jnp.bfloat16)
        k = _rope(jnp.dot(u, wk, preferred_element_type=jnp.float32).reshape(m, kt, HEAD_DIM), cs).astype(jnp.bfloat16)
        v = jnp.dot(u, wv, preferred_element_type=jnp.float32).astype(jnp.bfloat16).reshape(m, kt, HEAD_DIM)
        k = jnp.repeat(k, r, axis=1)
        v = jnp.repeat(v, r, axis=1)
        buf = jnp.concatenate([q.reshape(m, sp, qh, HEAD_DIM), k.reshape(m, sp, kd, HEAD_DIM), v.reshape(m, sp, kd, HEAD_DIM)], axis=2)
        buf = lax.all_to_all(buf.transpose(1, 0, 2, 3), "sp", 0, 0, tiled=True)
        buf = buf.reshape(n, qh + 2 * kd, HEAD_DIM)
        qa = buf[:, :qh]
        ka = buf[:, qh:qh + kd]
        va = buf[:, qh + kd:]
        att = _attention(qa.reshape(n, kd, qh // kd, HEAD_DIM), ka, va, 0)
        att = lax.all_to_all(att.reshape(sp, m, qh * HEAD_DIM), "sp", 0, 0, tiled=True)
        att = att.transpose(1, 0, 2).reshape(m, ht * HEAD_DIM)
        o = lax.psum(jnp.dot(att, wo, preferred_element_type=jnp.float32), "tp")
        x1 = (x.astype(jnp.float32) + o).astype(jnp.bfloat16)
        u2 = _rms(x1, g2)
        hid = (jax.nn.silu(jnp.dot(u2, w1, preferred_element_type=jnp.float32)) * jnp.dot(u2, w3, preferred_element_type=jnp.float32)).astype(jnp.bfloat16)
        mm = lax.psum(jnp.dot(hid, w2, preferred_element_type=jnp.float32), "tp")
        y = (x1.astype(jnp.float32) + mm).astype(jnp.bfloat16)
        return y, ka, va

    return jax.shard_map(
        local,
        mesh=mesh,
        in_specs=(tok, P(("rep", "sp")), P(), P(), col, col, col, row, col, col, row),
        out_specs=(tok, cache, cache),
        check_vma=False,
    )
```

profile of v0, /device:TPU:0, one launch (start us, length us, event | category | flops | bytes accessed | tf_op | source)
XLA Modules:
  0.0 1437.1 jit_solution(6244801337395284729)
XLA Ops:
  21.9 8.7 fusion.157
  35.5 21.7 %convolution_bitcast_fusion = f32[128,8,16,128]{3,1,2,0:T(8,128)S(1)} fusion(bf16[4096,2048]{1,0:T(8,128)(2,1)} %param.15, bf16[1024,4096]{1,0:T(8,128)(2,1)} %param.11, f32[4096]{0:T(1024)S(1)} %copy-done.27, f32[1024]{0:T(1024)S(1)} %add_rsqrt_fusion.1), kind=kOutput, calls=%fused_computation.78 | convolution fusion | flops 17196646400 | bytes 33574912 | tf_op jit(solution)/shard_map/dot_general | solution.py:68
  91.1 58.4 %all-to-all-done = bf16[4,1024,6,128]{3,1,2,0:T(8,128)(2,1)} async-done(((bf16[4,1024,6,128]{3,1,2,0:T(8,128)(2,1)}), bf16[4,1024,6,128]{3,1,2,0:T(8,128)(2,1)}, u32[]{:S(2)}, u32[]{:S(2)}) %all-to-all-start) | async-done | bytes 6291488 | tf_op jit(solution)/shard_map/all_to_all | solution.py:74
  166.2 9.5 fusion.23
  175.7 10.5 fusion.17
  186.2 11.8 fusion.5
  198.0 14.0 fusion.3
  211.9 16.2 %fusion.2 = (f32[4,512]{1,0:T(4,128)}, f32[4096,512,4]{1,0,2:T(8,128)}) fusion(pred[512,4096]{0,1:T(8,128)(4,1)} %iota_compare_fusion, bf16[4096,6,128]{2,0,1:T(8,128)(2,1)} %bitcast.414, bf16[4096,1,128]{2,0,1:T(8,128)(2,1)} %copy-done.24), kind=kOutput, calls=%fused_computation.9 | convolution fusion | flops 2172647424 | bytes 37232640 | tf_op jit(solution)/shard_map/qkgd,knd->kgqn/dot_general | solution.py:43
  256.5 9.8 fusion.110
  280.8 11.3 fusion.4
  292.1 13.1 fusion.98
  305.3 12.8 fusion.1
  318.1 14.6 %fusion.92 = bf16[4096,1,4,128]{0,3,2,1:T(8,128)(2,1)} fusion(bf16[4096,1,4,128]{0,3,2,1:T(8,128)(2,1)} %fusion.98, f32[4,512]{1,0:T(4,128)S(1)} %fusion.1, f32[4,512]{1,0:T(4,128)S(1)} %copy-done.25, f32[3584,512,4]{1,0,2:T(8,128)} %get-tuple-element.28, pred[512,3584]{0,1:T(8,128)(4,1)S(1)} %copy-done.7, bf16[1,4096,128]{2,1,0:T(8,128)(2,1)S(1)} %bitcast.426), kind=kOutput, calls=%fused_computation.104 | convolution fusion | flops 1916010496 | bytes 32653312 | tf_op jit(solution)/shard_map/kgqn,knd->qkgd/dot_general | solution.py:47
  332.7 14.6 %fusion = f32[4,512]{1,0:T(4,128)S(1)} fusion(f32[4096,512,4]{1,0,2:T(8,128)} %get-tuple-element.30, f32[4,512]{1,0:T(4,128)S(1)} %copy-done.26, pred[512,4096]{0,1:T(8,128)(4,1)S(1)} %copy-done.4), kind=kLoop, calls=%fused_computation.3 | loop fusion | flops 33552384 | bytes 35667968 | tf_op jit(solution)/shard_map/reduce_sum | solution.py:46
  347.3 16.1 %fusion.86 = bf16[4096,1,4,128]{0,3,2,1:T(8,128)(2,1)} fusion(bf16[4096,1,4,128]{0,3,2,1:T(8,128)(2,1)} %fusion.92, f32[4,512]{1,0:T(4,128)S(1)} %fusion, f32[4,512]{1,0:T(4,128)S(1)} %copy-done.26, f32[4096,512,4]{1,0,2:T(8,128)} %get-tuple-element.30, pred[512,4096]{0,1:T(8,128)(4,1)S(1)} %copy-done.4, bf16[4096,1,128]{2,0,1:T(8,128)(2,1)S(1)} %copy-done.23), kind=kOutput, calls=%fused_computation.102 | convolution fusion | flops 2189688832 | bytes 37240832 | tf_op jit(solution)/shard_map/kgqn,knd->qkgd/dot_general | solution.py:47
  374.8 50.7 %all_to_all.10 = bf16[4,1024,512]{1,2,0:T(8,128)(2,1)S(1)} all-to-all(bf16[4,1024,512]{1,2,0:T(8,128)(2,1)S(1)} %copy.82), channel_id=1, replica_groups=mesh['rep'=1,'tp'=2,'sp'=4] {'sp'}, dimensions={0} | all-to-all | bytes 8388608 | tf_op jit(solution)/shard_map/all_to_all | solution.py:80
  425.5 22.9 %fusion.163 = f32[1024,4096]{1,0:T(8,128)} fusion(bf16[1024,2048]{0,1:T(8,128)(2,1)S(1)} %bitcast.417, bf16[2048,4096]{1,0:T(8,128)(2,1)} %param.18), kind=kOutput, calls=%fused_computation.180 | convolution fusion | flops 17179869184 | bytes 37748736 | tf_op jit(solution)/shard_map/dot_general | solution.py:82
  448.4 373.1 %all-reduce.3.cloned.1.call-done = f32[1024,4096]{1,0:T(8,128)} async-done(((f32[1024,4096]{1,0:T(8,128)}), f32[1024,4096]{1,0:T(8,128)}) %all-reduce.3.cloned.1.call-update) | async-done | bytes 16777232 | tf_op jit(solution)/shard_map/psum | solution.py:82
  821.5 9.4 fusion.11
  834.3 67.9 %fusion.42 = f32[1024,7168]{1,0:T(8,128)} fusion(bf16[4096,7168]{1,0:T(8,128)(2,1)} %param.19, bf16[1024,4096]{1,0:T(8,128)(2,1)S(1)} %get-tuple-element.4, f32[4096]{0:T(1024)S(1)} %copy-done.28, f32[1024]{0:T(1024)S(1)} %add_rsqrt_fusion), kind=kOutput, calls=%fused_computation.81 | convolution fusion | flops 60146319360 | bytes 96489472 | tf_op jit(solution)/shard_map/dot_general | solution.py:85
  902.2 72.8 %multiply_convert_fusion.clone.4 = bf16[1024,7168]{1,0:T(8,128)(2,1)} fusion(f32[1024,7168]{1,0:T(8,128)} %fusion.42, bf16[4096,7168]{1,0:T(8,128)(2,1)} %param.20, bf16[1024,4096]{1,0:T(8,128)(2,1)} %copy-done.1, f32[4096]{0:T(1024)S(1)} %copy-done.28, f32[1024]{0:T(1024)S(1)} %add_rsqrt_fusion), kind=kOutput, calls=%fused_computation.5.clone.clone.clone.1 | convolution fusion | flops 60190359552 | bytes 111169536 | tf_op jit(solution)/shard_map/dot_general | solution.py:85
  975.0 70.4 %fusion.18 = f32[1024,4096]{1,0:T(8,128)} fusion(bf16[7168,4096]{1,0:T(8,128)(2,1)} %param.21, bf16[1024,7168]{1,0:T(8,128)(2,1)} %multiply_convert_fusion.clone.4), kind=kOutput, calls=%fused_computation.40 | convolution fusion | flops 60129542144 | bytes 90177536 | tf_op jit(solution)/shard_map/dot_general | solution.py:86
  1045.4 372.6 %all-reduce.5.cloned.1.call-done = f32[1024,4096]{1,0:T(8,128)} async-done(((f32[1024,4096]{1,0:T(8,128)}), f32[1024,4096]{1,0:T(8,128)}) %all-reduce.5.cloned.1.call-update) | async-done | bytes 16777232 | tf_op jit(solution)/shard_map/psum | solution.py:86
  1418.0 12.0 fusion.14
  (136 shorter events, 127.6 us)
Async XLA Ops:
  72.9 76.6 %all-to-all-start = ((bf16[4,1024,6,128]{3,1,2,0:T(8,128)(2,1)}), bf16[4,1024,6,128]{3,1,2,0:T(8,128)(2,1)}, u32[]{:S(2)}, u32[]{:S(2)}) async-start(bf16[4,1024,6,128]{3,1,2,0:T(8,128)(2,1)} %maximum_bitcast_fusion), calls=%async_computation | async-start | bytes 12582912 | tf_op jit(solution)/shard_map/all_to_all | solution.py:74
  78.1 743.4 %all-reduce.3.cloned.1.call-start = ((), (), s32[]{:S(2)}) async-start(), calls=%async_computation.2 | async-start | bytes 33554432 | tf_op jit(solution)/shard_map/psum | solution.py:82
  78.3 75.7 %copy-start.19 = (pred[512,512]{0,1:T(8,128)(4,1)}, pred[512,512]{0,1:T(8,128)(4,1)S(1)}, u32[]{:S(2)}) copy-start(pred[512,512]{0,1:T(8,128)(4,1)S(1)} %iota_compare_fusion.7) | copy-start | bytes 786436
  78.7 78.7 %copy-start.17 = (pred[512,1024]{0,1:T(8,128)(4,1)}, pred[512,1024]{0,1:T(8,128)(4,1)S(1)}, u32[]{:S(2)}) copy-start(pred[512,1024]{0,1:T(8,128)(4,1)S(1)} %iota_compare_fusion.6) | copy-start | bytes 1572868
  88.1 109.9 %copy-start.6 = (pred[512,3584]{0,1:T(8,128)(4,1)}, pred[512,3584]{0,1:T(8,128)(4,1)S(1)}, u32[]{:S(2)}) copy-start(pred[512,3584]{0,1:T(8,128)(4,1)S(1)} %iota_compare_fusion.1) | copy-start | bytes 5505028
  154.0 32.2 %copy-start.24 = (bf16[4096,1,128]{2,0,1:T(8,128)(2,1)}, bf16[4096,1,128]{2,0,1:T(8,128)(2,1)S(1)}, u32[]{:S(2)}) copy-start(bf16[4096,1,128]{2,0,1:T(8,128)(2,1)S(1)} %get-tuple-element.8) | copy-start | bytes 3145732
  166.2 75.2 %copy-start.2 = (f32[1536,512,4]{1,0,2:T(8,128)}, f32[1536,512,4]{1,0,2:T(8,128)S(1)}, u32[]{:S(2)}) copy-start(f32[1536,512,4]{1,0,2:T(8,128)S(1)} %get-tuple-element.20) | copy-start | bytes 37748740
  175.7 10.5 copy-start.8
  211.9 16.2 %copy-start.20 = (pred[512,512]{0,1:T(8,128)(4,1)S(1)}, pred[512,512]{0,1:T(8,128)(4,1)}, u32[]{:S(2)}) copy-start(pred[512,512]{0,1:T(8,128)(4,1)} %copy-done.19) | copy-start | bytes 786436
  211.9 19.4 %copy-start.21 = (bf16[4096,1,128]{2,0,1:T(8,128)(2,1)S(1)}, bf16[4096,1,128]{2,0,1:T(8,128)(2,1)}, u32[]{:S(2)}) copy-start(bf16[4096,1,128]{2,0,1:T(8,128)(2,1)} %get-tuple-element.7) | copy-start | bytes 3145732
  241.4 10.7 slice-start.5
  252.8 13.5 slice-start
  256.5 9.8 slice-start.1
  256.5 9.8 slice-start.2
  256.5 9.8 slice-start.3
  256.5 10.8 slice-start.4
  256.5 11.1 copy-start.11
  280.8 11.3 copy-start.23
  292.1 13.2 copy-start.7
  292.1 13.2 copy-start.25
  318.1 14.6 %copy-start.4 = (pred[512,4096]{0,1:T(8,128)(4,1)S(1)}, pred[512,4096]{0,1:T(8,128)(4,1)}, u32[]{:S(2)}) copy-start(pred[512,4096]{0,1:T(8,128)(4,1)} %iota_compare_fusion) | copy-start | bytes 6291460
  318.1 14.6 %copy-start.26 = (f32[4,512]{1,0:T(4,128)S(1)}, f32[4,512]{1,0:T(4,128)}, u32[]{:S(2)}) copy-start(f32[4,512]{1,0:T(4,128)} %get-tuple-element.29) | copy-start | bytes 24580
  448.4 385.9 %copy-start.28 = (f32[4096]{0:T(1024)S(1)}, f32[4096]{0:T(1024)}, u32[]{:S(2)}) copy-start(f32[4096]{0:T(1024)} %param.14) | copy-start | bytes 49156
  448.4 969.6 %all-reduce.5.cloned.1.call-start = ((), (), s32[]{:S(2)}) async-start(), calls=%async_computation.3 | async-start | bytes 33554432 | tf_op jit(solution)/shard_map/psum | solution.py:86
  (19 other events, 112.3 us)
Sparse Core Ops, SparseCore 0:
  448.5 372.9 all-reduce.2
  1045.5 372.4 all-reduce.4
where the time goes:
time: 1440 us
  waiting for transfers between devices  804 us (56%)
  matrix products  423 us (29%)
  other arithmetic  107 us (7%)
  blocking collectives  50.7 us (4%)
  local copies, waits for them, and re-layouts  32 us (2%)
  between operations  14.8 us (1%)
    psum x1, waiting for transfers between devices, local(): o = lax.psum(jnp.dot(att, wo, preferred_element_type=jnp.float32), 'tp')  373 us
    psum x1, waiting for transfers between devices, local(): mm = lax.psum(jnp.dot(hid, w2, preferred_element_type=jnp.float32), 'tp')  373 us
    dot_general x8, matrix products, _attention(): jnp.einsum('kgqn,knd->qkgd', p, vh[:, :hi], preferred_element_type=jnp.fl...  78.2 us
    dot_general x8, matrix products, _attention(): jnp.einsum('qkgd,knd->kgqn', q[i * bq:(i + 1) * bq], kh[:, :hi], preferre...  74 us
    dot_general x1, matrix products, local(): jnp.dot(u2, w3, preferred_element_type=jnp.float32)  72.8 us
    dot_general x1, matrix products, local(): mm = lax.psum(jnp.dot(hid, w2, preferred_element_type=jnp.float32), 'tp')  70.4 us
    dot_general x1, matrix products, local(): jnp.dot(u2, w1, preferred_element_type=jnp.float32)  67.9 us
    all_to_all x1, waiting for transfers between devices, local(): buf = lax.all_to_all(buf.transpose(1, 0, 2, 3), 'sp', 0, 0, tiled=True)  58.4 us
  transfers between devices with their start and end apart: 3, of which 3 were waited for; matrix products, arithmetic and copies ran while one was open for 1% of the time, Pallas kernels for 0%

commit v1 on v0

v1 whole, which is shorter than its diff:
```python
import functools

import jax
import jax.numpy as jnp
from jax import lax
from jax.experimental import pallas as pl
from jax.experimental.pallas import tpu as pltpu
from jax.sharding import PartitionSpec as P

HEAD_DIM = 128
EPS = 1e-5
ROPE_BASE = 5e5
SCALE_LOG2E = HEAD_DIM ** -0.5 * 1.4426950408889634
NEG = -1e30
BQ = 512
BK = 1024
MESH = pl.DeviceIdType.MESH
F32 = jnp.float32
BF16 = jnp.bfloat16


def _rms(x, g):
    x32 = x.astype(F32)
    r = lax.rsqrt(jnp.mean(x32 * x32, axis=-1, keepdims=True) + EPS)
    return (x32 * r * g).astype(BF16)


def _tables(pos):
    half = HEAD_DIM // 2
    inv = ROPE_BASE ** (-2.0 * jnp.arange(half, dtype=F32) / HEAD_DIM)
    ang = pos.astype(F32)[:, None] * inv
    c, s = jnp.cos(ang), jnp.sin(ang)
    return jnp.concatenate([c, c], axis=1), jnp.concatenate([-s, s], axis=1)


def _barrier(peers):
    sem = pltpu.get_barrier_semaphore()
    for p in peers:
        pl.semaphore_signal(sem, inc=1, device_id=p, device_id_type=MESH)
    pl.semaphore_wait(sem, len(peers))


def _sp_order(s):
    return [(s + 2) % 4, 3 - s, s + 1 - 2 * (s % 2), s]


def _qkv_body(x_hbm, g_ref, cos_ref, sin_ref, wq_hbm, wk_hbm, wv_hbm, q_hbm, k_hbm, v_hbm,
              xbuf, u, wq, wkv, qo, ko, vo, xsem, wsem, ssem, rsem, lsem):
    rep, tp, s = lax.axis_index("rep"), lax.axis_index("tp"), lax.axis_index("sp")
    order = _sp_order(s)
    m = u.shape[0]
    nb = xbuf.shape[0]
    rows = m // nb
    hm = m // 2
    qw = qo.shape[2]

    def wcopies(t):
        j = order[t]
        sl = t % 2
        return [
            pltpu.make_async_copy(wq_hbm.at[:, pl.ds(pl.multiple_of(j * qw, 128), qw)], wq.at[sl], wsem.at[sl, 0]),
            pltpu.make_async_copy(wk_hbm.at[:, pl.ds(pl.multiple_of(j * 128, 128), 128)], wkv.at[sl, :, pl.ds(0, 128)], wsem.at[sl, 1]),
            pltpu.make_async_copy(wv_hbm.at[:, pl.ds(pl.multiple_of(j * 128, 128), 128)], wkv.at[sl, :, pl.ds(128, 128)], wsem.at[sl, 2]),
        ]

    xc = [pltpu.make_async_copy(x_hbm.at[pl.ds(b * rows, rows), :], xbuf.at[b], xsem.at[b]) for b in range(nb)]
    for c in xc[:2]:
        c.start()
    for c in wcopies(0):
        c.start()
    for c in xc[2:]:
        c.start()
    for c in wcopies(1):
        c.start()
    _barrier([(rep, tp, j) for j in order[:3]])
    for b in range(nb):
        xc[b].wait()

        @pl.loop(0, rows // 64)
        def _(i, b=b):
            xs = xbuf[b, pl.ds(pl.multiple_of(i * 64, 64), 64), :].astype(F32)
            r = lax.rsqrt(jnp.mean(xs * xs, axis=-1, keepdims=True) + EPS)
            u[pl.ds(pl.multiple_of(b * rows + i * 64, 64), 64), :] = (xs * r * g_ref[...]).astype(BF16)

    def rope(t, r0):
        c = cos_ref[pl.ds(r0, t.shape[0]), :]
        sn = sin_ref[pl.ds(r0, t.shape[0]), :]
        return t * c + pltpu.roll(t, 64, 1) * sn

    def pieces(t, h):
        j = order[t]
        dst = pl.ds(pl.multiple_of(s * m + h * hm, hm), hm)
        src = pl.ds(h * hm, hm)
        trip = [(qo.at[t, src, :], q_hbm.at[dst, :]), (ko.at[t, src, :], k_hbm.at[dst, :]), (vo.at[t, src, :], v_hbm.at[dst, :])]
        if t == 3:
            return [pltpu.make_async_copy(a, b, lsem.at[h, i]) for i, (a, b) in enumerate(trip)]
        return [pltpu.make_async_remote_copy(src_ref=a, dst_ref=b, send_sem=ssem.at[t, h, i], recv_sem=rsem.at[t, h, i],
                                             device_id=(rep, tp, j), device_id_type=MESH) for i, (a, b) in enumerate(trip)]

    for t in range(4):
        sl = t % 2
        for c in wcopies(t):
            c.wait()
        for h in range(2):
            @pl.loop(0, hm // 256)
            def _(i, t=t, h=h, sl=sl):
                r0 = pl.multiple_of(h * hm + i * 256, 256)
                ub = u[pl.ds(r0, 256), :]
                qq = jnp.dot(ub, wq[sl], preferred_element_type=F32)
                for n in range(qw // 128):
                    qo[t, pl.ds(r0, 256), n * 128:(n + 1) * 128] = rope(qq[:, n * 128:(n + 1) * 128], r0).astype(BF16)
                kv = jnp.dot(ub, wkv[sl], preferred_element_type=F32)
                ko[t, pl.ds(r0, 256), :] = rope(kv[:, :128], r0).astype(BF16)
                vo[t, pl.ds(r0, 256), :] = kv[:, 128:].astype(BF16)
            for c in pieces(t, h):
                c.start()
        if t < 2:
            for c in wcopies(t + 2):
                c.start()
    for h in range(2):
        for c in pieces(3, h):
            c.wait()
    for t in range(3):
        for h in range(2):
            for c in pieces(t, h):
                c.wait()


def _qkv(x, g1, cos, sin, wq, wk, wv, n):
    m, d = x.shape
    qw = wq.shape[1] // 4
    any_ = pl.BlockSpec(memory_space=pl.ANY)
    vm = pl.BlockSpec(memory_space=pltpu.VMEM)
    return pl.pallas_call(
        _qkv_body,
        in_specs=[any_, vm, vm, vm, any_, any_, any_],
        out_specs=[any_, any_, any_],
        out_shape=[jax.ShapeDtypeStruct((n, qw), BF16), jax.ShapeDtypeStruct((n, 128), BF16), jax.ShapeDtypeStruct((n, 128), BF16)],
        scratch_shapes=[
            pltpu.VMEM((4, m // 4, d), BF16),
            pltpu.VMEM((m, d), BF16),
            pltpu.VMEM((2, d, qw), BF16),
            pltpu.VMEM((2, d, 256), BF16),
            pltpu.VMEM((4, m, qw), BF16),
            pltpu.VMEM((4, m, 128), BF16),
            pltpu.VMEM((4, m, 128), BF16),
            pltpu.SemaphoreType.DMA((4,)),
            pltpu.SemaphoreType.DMA((2, 3)),
            pltpu.SemaphoreType.DMA((3, 2, 3)),
            pltpu.SemaphoreType.DMA((3, 2, 3)),
            pltpu.SemaphoreType.DMA((2, 3)),
        ],
        compiler_params=pltpu.CompilerParams(collective_id=1, has_side_effects=True, vmem_limit_bytes=56 * 2**20),
        cost_estimate=pl.CostEstimate(flops=2 * m * d * (4 * qw + 1024), bytes_accessed=80 * 2**20, transcendentals=0),
        name="qkv_exchange",
    )(x, g1.reshape(1, -1), cos, sin, wq, wk, wv)


def _attn_body(q_ref, k_ref, v_ref, own_hbm, oth_hbm, vt, acc, ms, ls, ob, ssem, rsem, lsem):
    rep, tp, s = lax.axis_index("rep"), lax.axis_index("tp"), lax.axis_index("sp")
    step = pl.program_id(0)
    i = (step % 2) * 4 + step // 2
    nh = q_ref.shape[1] // 128
    order = _sp_order(s)

    @pl.when(step == 0)
    def _():
        _barrier([(rep, tp, j) for j in order[:3]] + [(rep, 1 - tp, j) for j in range(4)])

        @pl.loop(0, k_ref.shape[0] // 512)
        def _(j):
            r0 = pl.multiple_of(j * 512, 512)
            vt[:, pl.ds(r0, 512)] = v_ref[pl.ds(r0, 512), :].T

    ms[...] = jnp.full_like(ms, NEG)
    ls[...] = jnp.zeros_like(ls)
    acc[...] = jnp.zeros_like(acc)

    def blk(k0, n, masked):
        k0 = pl.multiple_of(k0, BQ)
        kb = k_ref[pl.ds(k0, n), :]
        vb = vt[:, pl.ds(k0, n)]

        def scores(h):
            return lax.dot_general(kb, q_ref[:, h * 128:(h + 1) * 128], (((1,), (1,)), ((), ())), preferred_element_type=F32)

        sc = scores(0)
        for h in range(nh):
            nxt = scores(h + 1) if h < nh - 1 else None
            if masked:
                kk = lax.broadcasted_iota(jnp.int32, (n, BQ), 0)
                qq = lax.broadcasted_iota(jnp.int32, (n, BQ), 1) + (i * BQ - k0)
                sc = jnp.where(qq >= kk, sc, NEG)
            m0 = ms[h:h + 1, :]
            m1 = jnp.maximum(m0, jnp.max(sc, axis=0, keepdims=True))
            p = jnp.exp2(sc * SCALE_LOG2E - m1 * SCALE_LOG2E)
            a = jnp.exp2((m0 - m1) * SCALE_LOG2E)
            ms[h:h + 1, :] = m1
            ls[h:h + 1, :] = ls[h:h + 1, :] * a + jnp.sum(p, axis=0, keepdims=True)
            acc[h] = acc[h] * a + jnp.dot(vb, p.astype(BF16), preferred_element_type=F32)
            sc = nxt

    start = i * BQ

    @pl.loop(0, start // BK)
    def _(j):
        blk(j * BK, BK, False)

    @pl.when(start % BK != 0)
    def _():
        blk(start - BQ, BQ, False)

    blk(start, BQ, True)
    for h in range(nh):
        o = acc[h] * (1.0 / ls[h:h + 1, :])
        ob[step, :, h * 128:(h + 1) * 128] = o.T.astype(BF16)

    w = q_ref.shape[1]

    def dst(ref, slot, src_s):
        return ref.at[slot, :, pl.ds(pl.multiple_of(src_s * w, 128), w)]

    def to_own(step):
        b = (step % 2) * 4 + step // 2
        d, half = b // 2, b % 2
        slot = (half + tp + 1) % 2
        return d, slot, pltpu.make_async_remote_copy(
            src_ref=ob.at[step], dst_ref=dst(own_hbm, slot, s), send_sem=ssem.at[0, step], recv_sem=rsem.at[0, s, slot],
            device_id=(rep, tp, d), device_id_type=MESH)

    def to_local(step):
        b = (step % 2) * 4 + step // 2
        half = b % 2
        slot = (half + tp + 1) % 2
        return pltpu.make_async_copy(ob.at[step], dst(own_hbm, slot, s), lsem.at[half])

    def to_oth(step):
        b = (step % 2) * 4 + step // 2
        d, half = b // 2, b % 2
        slot = (half + 1 - tp + 1) % 2
        return pltpu.make_async_remote_copy(
            src_ref=ob.at[step], dst_ref=dst(oth_hbm, slot, s), send_sem=ssem.at[1, step], recv_sem=rsem.at[1, s, slot],
            device_id=(rep, 1 - tp, d), device_id_type=MESH)

    to_oth(step).start()
    mine = i // 2 == s

    @pl.when(mine)
    def _():
        to_local(step).start()

    @pl.when(jnp.logical_not(mine))
    def _():
        to_own(step)[2].start()

    @pl.when(step == pl.num_programs(0) - 1)
    def _():
        @pl.loop(0, 8)
        def _(t):
            to_oth(t).wait_send()
            b = (t % 2) * 4 + t // 2

            @pl.when(b // 2 == s)
            def _():
                to_local(t).wait()

            @pl.when(b // 2 != s)
            def _():
                to_own(t)[2].wait_send()

        @pl.loop(0, 4)
        def _(j):
            @pl.loop(0, 2)
            def _(slot):
                pltpu.make_async_remote_copy(
                    src_ref=ob.at[0], dst_ref=dst(oth_hbm, slot, j), send_sem=ssem.at[1, 0], recv_sem=rsem.at[1, j, slot],
                    device_id=(rep, 1 - tp, j), device_id_type=MESH).wait_recv()

                @pl.when(j != s)
                def _():
                    pltpu.make_async_remote_copy(
                        src_ref=ob.at[0], dst_ref=dst(own_hbm, slot, j), send_sem=ssem.at[0, 0], recv_sem=rsem.at[0, j, slot],
                        device_id=(rep, tp, j), device_id_type=MESH).wait_recv()


def _attention(q, k, v):
    n, w = q.shape
    nh = w // 128
    any_ = pl.BlockSpec(memory_space=pl.ANY)
    full = pl.BlockSpec((n, 128), lambda t: (0, 0))
    shape = jax.ShapeDtypeStruct((2, BQ, 4 * w), BF16)
    return pl.pallas_call(
        _attn_body,
        grid=(n // BQ,),
        in_specs=[pl.BlockSpec((BQ, w), lambda t: ((t % 2) * 4 + t // 2, 0)), full, full],
        out_specs=[any_, any_],
        out_shape=[shape, shape],
        scratch_shapes=[
            pltpu.VMEM((128, n), BF16),
            pltpu.VMEM((nh, 128, BQ), F32),
            pltpu.VMEM((8, BQ), F32),
            pltpu.VMEM((8, BQ), F32),
            pltpu.VMEM((n // BQ, BQ, w), BF16),
            pltpu.SemaphoreType.DMA((2, 8)),
            pltpu.SemaphoreType.DMA((2, 4, 2)),
            pltpu.SemaphoreType.DMA((2,)),
        ],
        compiler_params=pltpu.CompilerParams(collective_id=2, has_side_effects=True, vmem_limit_bytes=56 * 2**20),
        cost_estimate=pl.CostEstimate(flops=2 * n * n * w * 2, bytes_accessed=16 * 2**20, transcendentals=0),
        name="attention_exchange",
    )(q, k, v)


NWO, NHID, NW2 = 8, 28, 16
UNITS = NWO + NHID + NW2
NBUF = 3
MB = 256


def _mlp_body(chunks, own_hbm, oth_hbm, x_hbm, wo_hbm, p0, p1, p2, p3, g_ref, w1_hbm, w3_hbm, w2_hbm, y_hbm,
              wb, abuf, xbuf, hid, pbuf, rbuf, ybuf, wsem, asem, ssem, rsem, ysem, yrsem, ylsem):
    rep, tp, s = lax.axis_index("rep"), lax.axis_index("tp"), lax.axis_index("sp")
    hr = wo_hbm.shape[0]
    qr = hr // 4
    hm = x_hbm.shape[0] // 2
    kh = w2_hbm.shape[0] // 2
    total = UNITS * len(chunks)
    s1 = s + 1 - 2 * (s % 2)
    quarters = [(p0, s), (p1, (s + 2) % 4), (p2, s1), (p3, (s1 + 2) % 4)]
    partner = (rep, 1 - tp, s)

    def col(j, w):
        return pl.ds(pl.multiple_of(j * w, w), w)

    def wo_copies(j, sl):
        cs = [pltpu.make_async_copy(wo_hbm.at[:, col(j, 512)], wb.at[sl, pl.ds(0, hr), :], wsem.at[sl, 0])]
        for n, (p, r) in enumerate(quarters):
            cs.append(pltpu.make_async_copy(p.at[:, col(j, 512)], wb.at[sl, pl.ds(pl.multiple_of(hr + r * qr, qr), qr), :], wsem.at[sl, n + 1]))
        return cs

    def hid_copies(j, sl):
        return [pltpu.make_async_copy(w1_hbm.at[:, col(j, 256)], wb.at[sl, :, pl.ds(0, 256)], wsem.at[sl, 0]),
                pltpu.make_async_copy(w3_hbm.at[:, col(j, 256)], wb.at[sl, :, pl.ds(256, 256)], wsem.at[sl, 1])]

    def w2_copies(t, sl):
        return [pltpu.make_async_copy(w2_hbm.at[pl.ds(pl.multiple_of(t % 2 * kh, 128), kh), col(t // 2, 512)], wb.at[sl, pl.ds(0, kh), :], wsem.at[sl, 0])]

    def issue(g):
        sl, u = g % NBUF, g % UNITS

        @pl.when(g < total)
        def _():
            @pl.when(u < NWO)
            def _():
                for c in wo_copies(u, sl):
                    c.start()

            @pl.when((u >= NWO) & (u < NWO + NHID))
            def _():
                for c in hid_copies(u - NWO, sl):
                    c.start()

            @pl.when(u >= NWO + NHID)
            def _():
                for c in w2_copies(u - NWO - NHID, sl):
                    c.start()

    def acts(c):
        slot, r0, nr = chunks[c]
        base = hm * ((tp + slot + 1) % 2) + r0
        rs = pl.ds(0, nr)
        return (pltpu.make_async_copy(x_hbm.at[pl.ds(pl.multiple_of(base, 128), nr), :], xbuf.at[rs, :], asem.at[0]),
                [pltpu.make_async_copy(own_hbm.at[slot, pl.ds(r0, nr), :], abuf.at[rs, pl.ds(0, hr)], asem.at[1]),
                 pltpu.make_async_copy(oth_hbm.at[slot, pl.ds(r0, nr), :], abuf.at[rs, pl.ds(hr, hr)], asem.at[2])])

    for g in range(NBUF - 1):
        issue(g)
    xc, ac = acts(0)
    xc.start()
    for c in ac:
        c.start()
    _barrier([partner])

    def send(ci, j):
        slot, r0, nr = chunks[ci]
        return pltpu.make_async_remote_copy(src_ref=pbuf.at[j, pl.ds(r0, nr), :], dst_ref=rbuf.at[j, pl.ds(r0, nr), :],
                                            send_sem=ssem.at[ci, j], recv_sem=rsem.at[ci, j], device_id=partner, device_id_type=MESH)

    yr0 = pl.multiple_of(tp * hm, 128)

    def ysend(j):
        return pltpu.make_async_remote_copy(src_ref=ybuf.at[j], dst_ref=y_hbm.at[pl.ds(yr0, hm), col(j, 512)],
                                            send_sem=ysem.at[j], recv_sem=yrsem.at[j], device_id=partner, device_id_type=MESH)

    def yrecv(j):
        return pltpu.make_async_remote_copy(src_ref=ybuf.at[j], dst_ref=y_hbm.at[pl.ds(pl.multiple_of((1 - tp) * hm, 128), hm), col(j, 512)],
                                            send_sem=ysem.at[j], recv_sem=yrsem.at[j], device_id=partner, device_id_type=MESH)

    def yown(j):
        return pltpu.make_async_copy(ybuf.at[j], y_hbm.at[pl.ds(yr0, hm), col(j, 512)], ylsem.at[j])

    nsend = len(chunks) - 1
    for ci, (slot, r0, nr) in enumerate(chunks):
        g0 = ci * UNITS
        xc, ac = acts(ci)
        xc.wait()
        for c in ac:
            c.wait()

        @pl.loop(0, NWO)
        def _(j, g0=g0, nr=nr):
            g = g0 + j
            sl = g % NBUF
            issue(g + NBUF - 1)
            for c in wo_copies(j, sl):
                c.wait()
            for b in range(nr // MB):
                rs = pl.ds(b * MB, MB)
                o = jnp.dot(abuf[rs, :], wb[sl], preferred_element_type=F32)
                xbuf[rs, col(j, 512)] = (xbuf[rs, col(j, 512)].astype(F32) + o).astype(BF16)

        @pl.loop(0, nr // 64)
        def _(i):
            rs = pl.ds(pl.multiple_of(i * 64, 64), 64)
            xs = xbuf[rs, :].astype(F32)
            r = lax.rsqrt(jnp.mean(xs * xs, axis=-1, keepdims=True) + EPS)
            abuf[rs, :] = (xs * r * g_ref[...]).astype(BF16)

        if ci + 1 < len(chunks):
            acts(ci + 1)[0].start()

        @pl.loop(0, NHID)
        def _(j, g0=g0, nr=nr):
            g = g0 + NWO + j
            sl = g % NBUF
            issue(g + NBUF - 1)
            for c in hid_copies(j, sl):
                c.wait()
            for b in range(nr // MB):
                rs = pl.ds(b * MB, MB)
                ab = jnp.dot(abuf[rs, :], wb[sl], preferred_element_type=F32)
                a = ab[:, :256]
                hid[rs, col(j, 256)] = (a / (1.0 + jnp.exp(-a)) * ab[:, 256:]).astype(BF16)

        if ci + 1 < len(chunks):
            for c in acts(ci + 1)[1]:
                c.start()

        @pl.loop(0, NW2 // 2)
        def _(j, g0=g0, ci=ci, slot=slot, r0=r0, nr=nr):
            g = g0 + NWO + NHID + 2 * j
            for h in range(2):
                sl = (g + h) % NBUF
                issue(g + h + NBUF - 1)
                for c in w2_copies(2 * j + h, sl):
                    c.wait()
                for b in range(nr // MB):
                    rs = pl.ds(b * MB, MB)
                    ps = pl.ds(r0 + b * MB, MB)
                    o = jnp.dot(hid[rs, h * kh:(h + 1) * kh], wb[sl, pl.ds(0, kh), :], preferred_element_type=F32)
                    if h == 0:
                        pbuf[j if slot == 0 else NW2 // 2, ps, :] = o
                    elif slot == 0:
                        pbuf[j, ps, :] = pbuf[j, ps, :] + o
                    else:
                        if b == 0:
                            for k in range(nsend):
                                send(k, j).wait_recv()
                        o = o + pbuf[NW2 // 2, ps, :] + rbuf[j, ps, :]
                        ybuf[j, ps, :] = (xbuf[rs, col(j, 512)].astype(F32) + o).astype(BF16)
            if slot == 0:
                send(ci, j).start()
            else:
                ysend(j).start()
                yown(j).start()

    @pl.loop(0, NW2 // 2)
    def _(j):
        for k in range(nsend):
            send(k, j).wait_send()
        ysend(j).wait_send()
        yown(j).wait()
        yrecv(j).wait_recv()


def _mlp(own, oth, x, wo, pieces, g2, w1, w3, w2):
    m, d = x.shape
    hm = m // 2
    chunks = ((0, 0, 256), (0, 256, 256), (1, 0, 512))
    any_ = pl.BlockSpec(memory_space=pl.ANY)
    vm = pl.BlockSpec(memory_space=pltpu.VMEM)
    nt = NW2 // 2
    return pl.pallas_call(
        functools.partial(_mlp_body, chunks),
        in_specs=[any_] * 8 + [vm] + [any_] * 3,
        out_specs=any_,
        out_shape=jax.ShapeDtypeStruct((m, d), BF16),
        scratch_shapes=[
            pltpu.VMEM((NBUF, d, 512), BF16),
            pltpu.VMEM((hm, d), BF16),
            pltpu.VMEM((hm, d), BF16),
            pltpu.VMEM((hm, w2.shape[0]), BF16),
            pltpu.VMEM((nt + 1, hm, 512), F32),
            pltpu.VMEM((nt, hm, 512), F32),
            pltpu.VMEM((nt, hm, 512), BF16),
            pltpu.SemaphoreType.DMA((NBUF, 5)),
            pltpu.SemaphoreType.DMA((3,)),
            pltpu.SemaphoreType.DMA((2, nt)),
            pltpu.SemaphoreType.DMA((2, nt)),
            pltpu.SemaphoreType.DMA((nt,)),
            pltpu.SemaphoreType.DMA((nt,)),
            pltpu.SemaphoreType.DMA((nt,)),
        ],
        compiler_params=pltpu.CompilerParams(collective_id=3, has_side_effects=True, vmem_limit_bytes=67043328),
        cost_estimate=pl.CostEstimate(flops=2 * m * d * (d + 3 * w1.shape[1]), bytes_accessed=640 * 2**20, transcendentals=0),
        name="mlp_sum",
    )(own, oth, x, wo, *pieces, g2.reshape(1, -1), w1, w3, w2)


def solution(mesh):
    tok = P(("rep", "sp"), None)
    col = P(None, "tp")
    row = P("tp", None)
    cache = P("rep", ("tp", "sp"), None)
    swap = [(0, 1), (1, 0)]

    def local(x, pos, g1, g2, wq, wk, wv, wo, w1, w3, w2):
        m, d = x.shape
        n = m * mesh.shape["sp"]
        s = lax.axis_index("sp")
        qr = wo.shape[0] // 4
        piece = lax.ppermute(lax.dynamic_slice(wo, (s * qr, 0), (qr, d)), "tp", swap)
        cos, sin = _tables(pos)
        q, k, v = _qkv(x, g1, cos, sin, wq, wk, wv, n)
        piece, q = lax.optimization_barrier((piece, q))
        far = lax.ppermute(piece, "sp", [(0, 2), (2, 0), (1, 3), (3, 1)])
        own, oth = _attention(q, k, v)
        far, own, oth = lax.optimization_barrier((far, own, oth))
        cross = [(0, 1), (1, 0), (2, 3), (3, 2)]
        near = lax.ppermute(piece, "sp", cross)
        near2 = lax.ppermute(far, "sp", cross)
        y = _mlp(own, oth, x, wo, (piece, far, near, near2), g2, w1, w3, w2)
        return y, k.reshape(n, 1, 128), v.reshape(n, 1, 128)

    return jax.shard_map(
        local,
        mesh=mesh,
        in_specs=(tok, P(("rep", "sp")), P(), P(), col, col, col, row, col, col, row),
        out_specs=(tok, cache, cache),
        check_vma=False,
    )
```

time: 1440 us -> 629 us (0.44)
  waiting for transfers between devices: 804 us -> 12.3 us
  Pallas kernels: 0 us -> 590 us
  matrix products: 423 us -> 0 us
  other arithmetic: 107 us -> 3.23 us
  blocking collectives: 50.7 us -> 0 us
  local copies, waits for them, and re-layouts: 32 us -> 16.6 us
    psum x2 -> x0, waiting for transfers between devices: 746 us -> none  [the longest x1 373 us: local(): o = lax.psum(jnp.dot(att, wo, preferred_element_type=jnp.float32), 'tp')]
    pallas_call x0 -> x3, Pallas kernels: none -> 590 us  [the longest x1 329 us: _mlp(): pl.pallas_call(functools.partial(_mlp_body, chunks), in_specs=[any_] * 8...]
    dot_general x23 -> x0, matrix products: 423 us -> none  [the longest x8 78.2 us: _attention(): jnp.einsum('kgqn,knd->qkgd', p, vh[:, :hi], preferred_element_type=jnp.fl...]
    reduce_sum x10 -> x0, other arithmetic: 69.6 us -> none  [the longest x8 54.7 us: _attention(): p = jax.nn.softmax(s, axis=-1).astype(jnp.bfloat16)]
    all_to_all x1 -> x0, waiting for transfers between devices: 58.4 us -> none  [local(): buf = lax.all_to_all(buf.transpose(1, 0, 2, 3), 'sp', 0, 0, tiled=True)]
    all_to_all x1 -> x0, blocking collectives: 50.7 us -> none  [local(): lax.all_to_all(att.reshape(sp, m, qh * HEAD_DIM), 'sp', 0, 0, tiled=True)]
    another operation x5 -> x0, local copies, waits for them, and re-layouts: 15 us -> none  [the longest x2 11.4 us: local(): att.reshape(sp, m, qh * HEAD_DIM)]
  transfers between devices with their start and end apart: 3 -> 4, of which waited for: 3 -> 2; matrix products, arithmetic and copies ran while one was open for 1% -> 1% of each run, Pallas kernels for 0% -> 42%
where the time goes in v1:
time: 629 us
  Pallas kernels  590 us (94%)
  local copies, waits for them, and re-layouts  16.6 us (3%)
  waiting for transfers between devices  12.3 us (2%)
    pallas_call x1, Pallas kernels, _mlp(): pl.pallas_call(functools.partial(_mlp_body, chunks), in_specs=[any_] * 8...  329 us
    pallas_call x1, Pallas kernels, _attention(): pl.pallas_call(_attn_body, grid=(n // BQ,), in_specs=[pl.BlockSpec((BQ, w...  179 us
    pallas_call x1, Pallas kernels, _qkv(): pl.pallas_call(_qkv_body, in_specs=[any_, vm, vm, vm, any_, any_, any_],...  81.8 us
    unnamed x13, local copies, waits for them, and re-layouts  14 us
  transfers between devices with their start and end apart: 4, of which 2 were waited for; matrix products, arithmetic and copies ran while one was open for 1% of the time, Pallas kernels for 42%

profile of v1, /device:TPU:0, one launch (start us, length us, event | category | flops | bytes accessed | tf_op | source)
XLA Modules:
  0.0 628.6 jit_solution(7829930822564317628)
XLA Ops:
  0.6 0.0 copy-start.2
  0.6 2.7 constant_dynamic-slice_fusion
  3.3 3.4 collective-permute-start
  6.7 0.0 copy-done.2
  6.7 1.9 fusion
  8.6 1.3 pad_maximum_fusion
  10.0 81.8 %qkv_exchange.1 = (bf16[4096,512]{1,0:T(8,128)(2,1)}, bf16[4096,128]{1,0:T(8,128)(2,1)}, bf16[4096,128]{1,0:T(8,128)(2,1)}) custom-call(bf16[1024,4096]{1,0:T(8,128)(2,1)} %x_hbm.3, f32[1,4096]{1,0:T(1,128)} %bitcast.6, f32[1024,128]{1,0:T(8,128)} %get-tuple-element.26.cos_ref, f32[1024,128]{1,0:T(8,128)} %get-tuple-element.27.sin_ref, ...), custom_call_target="tpu_custom_call" | custom-call | flops 25769803776 | bytes 83886080 | tf_op jit(solution)/shard_map/qkv_exchange/pallas_call | solution.py:134
  91.8 5.5 collective-permute-done.p0
  97.3 1.7 collective-permute-start.1
  99.0 0.0 collective-permute-start.2
  99.0 179.3 %attention_exchange.1 = (bf16[2,512,2048]{2,1,0:T(8,128)(2,1)}, bf16[2,512,2048]{2,1,0:T(8,128)(2,1)}) custom-call(bf16[4096,512]{1,0:T(8,128)(2,1)} %get-tuple-element.15.q_ref, bf16[4096,128]{1,0:T(8,128)(2,1)} %get-tuple-element.16.k_ref, bf16[4096,128]{1,0:T(8,128)(2,1)} %get-tuple-element.17.v_ref), custom_call_target="tpu_custom_call" | custom-call | flops 34359738368 | bytes 16777216 | tf_op jit(solution)/shard_map/attention_exchange/pallas_call | solution.py:292
  278.3 0.0 collective-permute-done.1.p1
  278.3 0.0 copy-start.3
  278.3 2.0 copy-done.3
  280.3 0.9 collective-permute-start.3
  281.2 0.0 collective-permute-done.2.p2
  281.2 6.8 %collective-permute-done.3.p3 = bf16[512,4096]{1,0:T(8,128)(2,1)S(1)} collective-permute-done((bf16[512,4096]{1,0:T(8,128)(2,1)S(1)}, bf16[512,4096]{1,0:T(8,128)(2,1)S(1)}, u32[]{:S(2)}, u32[]{:S(2)}) %collective-permute-start.3) | collective-permute-done | bytes 4194336 | tf_op jit(solution)/shard_map/ppermute | solution.py:541
  288.0 2.0 copy-done.4
  289.9 328.7 %mlp_sum.1 = bf16[1024,4096]{1,0:T(8,128)(2,1)} custom-call(bf16[2,512,2048]{2,1,0:T(8,128)(2,1)} %get-tuple-element.20.own_hbm, bf16[2,512,2048]{2,1,0:T(8,128)(2,1)} %get-tuple-element.21.oth_hbm, bf16[1024,4096]{1,0:T(8,128)(2,1)} %x_hbm.3, bf16[2048,4096]{1,0:T(8,128)(2,1)} %wo_hbm.1, bf16[512,4096]{1,0:T(8,128)(2,1)} %collective-permute-done.p0, ...), custom_call_target="tpu_custom_call" | custom-call | flops 214748364800 | bytes 671088640 | tf_op jit(solution)/shard_map/mlp_sum/pallas_call | solution.py:493
  618.6 0.0 copy-start.1
  618.6 0.0 copy-start
  618.6 8.0 %copy.17 = bf16[1024,4096]{1,0:T(8,128)(2,1)} copy(bf16[1024,4096]{1,0:T(8,128)(2,1)} %mlp_sum.1) | data formatting | bytes 16777216
  626.7 1.0 copy.18
  627.7 1.0 copy.19
  (5 shorter events, 0.0 us)
Async XLA Ops:
  0.6 6.1 copy-start.2
  3.3 94.0 %collective-permute-start = (bf16[512,4096]{1,0:T(8,128)(2,1)S(1)}, bf16[512,4096]{1,0:T(8,128)(2,1)}, u32[]{:S(2)}, u32[]{:S(2)}) collective-permute-start(bf16[512,4096]{1,0:T(8,128)(2,1)S(1)} %constant_dynamic-slice_fusion), channel_id=1, source_target_pairs={{0,4},{4,0},{1,5},{5,1},{2,6},{6,2},{3,7},{7,3}} | collective-permute-start | bytes 12582920 | tf_op jit(solution)/shard_map/ppermute | solution.py:532
  97.3 181.0 %collective-permute-start.1 = (bf16[512,4096]{1,0:T(8,128)(2,1)}, bf16[512,4096]{1,0:T(8,128)(2,1)S(1)}, u32[]{:S(2)}, u32[]{:S(2)}) collective-permute-start(bf16[512,4096]{1,0:T(8,128)(2,1)} %collective-permute-done.p0), channel_id=1, source_target_pairs={{0,2},{2,0},{1,3},{3,1},{4,6},{6,4},{5,7},{7,5}} | collective-permute-start | bytes 12582920 | tf_op jit(solution)/shard_map/ppermute | solution.py:536
  99.0 182.2 %collective-permute-start.2 = (bf16[512,4096]{1,0:T(8,128)(2,1)}, bf16[512,4096]{1,0:T(8,128)(2,1)}, u32[]{:S(2)}, u32[]{:S(2)}) collective-permute-start(bf16[512,4096]{1,0:T(8,128)(2,1)} %collective-permute-done.p0), channel_id=1, source_target_pairs={{0,1},{1,0},{2,3},{3,2},{4,5},{5,4},{6,7},{7,6}} | collective-permute-start | bytes 12582920 | tf_op jit(solution)/shard_map/ppermute | solution.py:540
  278.3 2.0 copy-start.3
  280.3 7.7 %collective-permute-start.3 = (bf16[512,4096]{1,0:T(8,128)(2,1)S(1)}, bf16[512,4096]{1,0:T(8,128)(2,1)S(1)}, u32[]{:S(2)}, u32[]{:S(2)}) collective-permute-start(bf16[512,4096]{1,0:T(8,128)(2,1)S(1)} %collective-permute-done.1.p1), channel_id=1, source_target_pairs={{0,1},{1,0},{2,3},{3,2},{4,5},{5,4},{6,7},{7,6}} | collective-permute-start | bytes 12582920 | tf_op jit(solution)/shard_map/ppermute | solution.py:541
  288.0 2.0 copy-start.4
  618.6 8.1 %copy-start.1 = (bf16[4096,128]{1,0:T(8,128)(2,1)S(1)}, bf16[4096,128]{1,0:T(8,128)(2,1)}, u32[]{:S(2)}) copy-start(bf16[4096,128]{1,0:T(8,128)(2,1)} %get-tuple-element.16.k_ref) | copy-start | bytes 3145732
  618.6 9.0 %copy-start = (bf16[4096,128]{1,0:T(8,128)(2,1)S(1)}, bf16[4096,128]{1,0:T(8,128)(2,1)}, u32[]{:S(2)}) copy-start(bf16[4096,128]{1,0:T(8,128)(2,1)} %get-tuple-element.17.v_ref) | copy-start | bytes 3145732

commit v2 on v1

--- a/solution.py
+++ b/solution.py
@@ -14,6 +14,8 @@
 NEG = -1e30
 BQ = 512
 BK = 1024
+WOP = 128
+WOY = 3
 MESH = pl.DeviceIdType.MESH
 F32 = jnp.float32
 BF16 = jnp.bfloat16
@@ -44,35 +46,49 @@
     return [(s + 2) % 4, 3 - s, s + 1 - 2 * (s % 2), s]
 
 
-def _qkv_body(x_hbm, g_ref, cos_ref, sin_ref, wq_hbm, wk_hbm, wv_hbm, q_hbm, k_hbm, v_hbm,
-              xbuf, u, wq, wkv, qo, ko, vo, xsem, wsem, ssem, rsem, lsem):
+def _wo_y(tp, s, rep, wo_hbm, wo_dst, ssem, rsem, k, nr):
+    r0 = pl.multiple_of(s * (wo_hbm.shape[0] // 4) + k * nr, 128)
+    return pltpu.make_async_remote_copy(src_ref=wo_hbm.at[pl.ds(r0, nr), :], dst_ref=wo_dst.at[pl.ds(r0, nr), :],
+                                        send_sem=ssem, recv_sem=rsem, device_id=(rep, 1 - tp, s), device_id_type=MESH)
+
+
+def _qkv_body(x_hbm, g_ref, cos_ref, sin_ref, wq_hbm, wk_hbm, wv_hbm, wo_hbm, q_hbm, k0_hbm, v0_hbm, k1_hbm, v1_hbm, wo_dst,
+              xbuf, u, wq, wkv, qo, ko, vo, xsem, wsem, ssem, rsem, lsem, qsem, qrsem, wosem, worsem):
     rep, tp, s = lax.axis_index("rep"), lax.axis_index("tp"), lax.axis_index("sp")
     order = _sp_order(s)
+    far, diag, mate = order[:3]
+    on_x0 = s // 2 == 0
     m = u.shape[0]
     nb = xbuf.shape[0]
     rows = m // nb
-    hm = m // 2
     qw = qo.shape[2]
 
-    def wcopies(t):
-        j = order[t]
-        sl = t % 2
+    def kvcopies(t):
+        j, sl = order[t], t % 2
         return [
-            pltpu.make_async_copy(wq_hbm.at[:, pl.ds(pl.multiple_of(j * qw, 128), qw)], wq.at[sl], wsem.at[sl, 0]),
             pltpu.make_async_copy(wk_hbm.at[:, pl.ds(pl.multiple_of(j * 128, 128), 128)], wkv.at[sl, :, pl.ds(0, 128)], wsem.at[sl, 1]),
             pltpu.make_async_copy(wv_hbm.at[:, pl.ds(pl.multiple_of(j * 128, 128), 128)], wkv.at[sl, :, pl.ds(128, 128)], wsem.at[sl, 2]),
         ]
 
+    groups = [mate, (mate + 2) % 4, s, far]
+
+    def qcopy(t):
+        return pltpu.make_async_copy(wq_hbm.at[:, pl.ds(pl.multiple_of(groups[t] * qw, 128), qw)], wq.at[t % 2], wsem.at[t % 2, 0])
+
     xc = [pltpu.make_async_copy(x_hbm.at[pl.ds(b * rows, rows), :], xbuf.at[b], xsem.at[b]) for b in range(nb)]
-    for c in xc[:2]:
+    xc[0].start()
+    for c in kvcopies(0):
         c.start()
-    for c in wcopies(0):
+    for c in xc[1:]:
         c.start()
-    for c in xc[2:]:
+    for c in kvcopies(1):
         c.start()
-    for c in wcopies(1):
+    qcopy(0).start()
+    qcopy(1).start()
+    _barrier([(rep, tp, far), (rep, tp, diag), (rep, tp, mate), (rep, 1 - tp, s)])
+    wo_sends = [_wo_y(tp, s, rep, wo_hbm, wo_dst, wosem.at[k], worsem.at[k], k, WOP) for k in range(WOY)]
+    for c in wo_sends:
         c.start()
-    _barrier([(rep, tp, j) for j in order[:3]])
     for b in range(nb):
         xc[b].wait()
 
@@ -87,55 +103,102 @@
         sn = sin_ref[pl.ds(r0, t.shape[0]), :]
         return t * c + pltpu.roll(t, 64, 1) * sn
 
-    def pieces(t, h):
-        j = order[t]
-        dst = pl.ds(pl.multiple_of(s * m + h * hm, hm), hm)
-        src = pl.ds(h * hm, hm)
-        trip = [(qo.at[t, src, :], q_hbm.at[dst, :]), (ko.at[t, src, :], k_hbm.at[dst, :]), (vo.at[t, src, :], v_hbm.at[dst, :])]
-        if t == 3:
-            return [pltpu.make_async_copy(a, b, lsem.at[h, i]) for i, (a, b) in enumerate(trip)]
-        return [pltpu.make_async_remote_copy(src_ref=a, dst_ref=b, send_sem=ssem.at[t, h, i], recv_sem=rsem.at[t, h, i],
-                                             device_id=(rep, tp, j), device_id_type=MESH) for i, (a, b) in enumerate(trip)]
-
+    dst = pl.ds(pl.multiple_of(s * m, 128), m)
+
+    def remote(t, sl, j):
+        pair = ((ko, k0_hbm), (vo, v0_hbm)) if sl == 0 else ((ko, k1_hbm), (vo, v1_hbm))
+        return [pltpu.make_async_remote_copy(src_ref=a.at[t], dst_ref=b.at[dst, :], send_sem=ssem.at[sl, t, i], recv_sem=rsem.at[sl, t, i],
+                                             device_id=(rep, tp, j), device_id_type=MESH) for i, (a, b) in enumerate(pair)]
+
+    def local(t, sl):
+        pair = ((ko, k0_hbm), (vo, v0_hbm)) if sl == 0 else ((ko, k1_hbm), (vo, v1_hbm))
+        return [pltpu.make_async_copy(a.at[t], b.at[dst, :], lsem.at[sl, i]) for i, (a, b) in enumerate(pair)]
+
+    sends = [[(0, far, False)], [(0, diag, False), (1, mate, False)], [(0, mate, False), (1, diag, True)], [(1, far, True)]]
     for t in range(4):
         sl = t % 2
-        for c in wcopies(t):
+        for c in kvcopies(t):
             c.wait()
-        for h in range(2):
-            @pl.loop(0, hm // 256)
-            def _(i, t=t, h=h, sl=sl):
-                r0 = pl.multiple_of(h * hm + i * 256, 256)
-                ub = u[pl.ds(r0, 256), :]
-                qq = jnp.dot(ub, wq[sl], preferred_element_type=F32)
-                for n in range(qw // 128):
-                    qo[t, pl.ds(r0, 256), n * 128:(n + 1) * 128] = rope(qq[:, n * 128:(n + 1) * 128], r0).astype(BF16)
-                kv = jnp.dot(ub, wkv[sl], preferred_element_type=F32)
-                ko[t, pl.ds(r0, 256), :] = rope(kv[:, :128], r0).astype(BF16)
-                vo[t, pl.ds(r0, 256), :] = kv[:, 128:].astype(BF16)
-            for c in pieces(t, h):
+
+        @pl.loop(0, m // 256)
+        def _(i, t=t, sl=sl):
+            r0 = pl.multiple_of(i * 256, 256)
+            kv = jnp.dot(u[pl.ds(r0, 256), :], wkv[sl], preferred_element_type=F32)
+            ko[t, pl.ds(r0, 256), :] = rope(kv[:, :128], r0).astype(BF16)
+            vo[t, pl.ds(r0, 256), :] = kv[:, 128:].astype(BF16)
+        for slot, j, x0_only in sends[t]:
+            def go(t=t, slot=slot, j=j):
+                for c in remote(t, slot, j):
+                    c.start()
+            if x0_only:
+                pl.when(on_x0)(go)
+            else:
+                go()
+        if t == 0 or t == 3:
+            for c in local(t, 1 if t == 0 else 0):
                 c.start()
         if t < 2:
-            for c in wcopies(t + 2):
+            for c in kvcopies(t + 2):
                 c.start()
-    for h in range(2):
-        for c in pieces(3, h):
-            c.wait()
-    for t in range(3):
-        for h in range(2):
-            for c in pieces(t, h):
-                c.wait()
-
-
-def _qkv(x, g1, cos, sin, wq, wk, wv, n):
+
+    qrow = pl.ds(pl.multiple_of(s % 2 * m, 128), m)
+
+    def qremote(t):
+        return pltpu.make_async_remote_copy(src_ref=qo.at[t], dst_ref=q_hbm.at[t % 2, qrow, :], send_sem=qsem.at[t], recv_sem=qrsem.at[t],
+                                            device_id=(rep, tp, mate), device_id_type=MESH)
+
+    def qlocal(t):
+        return pltpu.make_async_copy(qo.at[t], q_hbm.at[t % 2, qrow, :], qsem.at[t])
+
+    for t in range(4):
+        qcopy(t).wait()
+
+        @pl.loop(0, m // 256)
+        def _(i, t=t):
+            r0 = pl.multiple_of(i * 256, 256)
+            qq = jnp.dot(u[pl.ds(r0, 256), :], wq[t % 2], preferred_element_type=F32)
+            for n in range(qw // 128):
+                qo[t, pl.ds(r0, 256), n * 128:(n + 1) * 128] = rope(qq[:, n * 128:(n + 1) * 128], r0).astype(BF16)
+        (qremote(t) if t < 2 else qlocal(t)).start()
+        if t < 2:
+            qcopy(t + 2).start()
+
+    for t in range(2):
+        qremote(t).wait()
+        qlocal(t + 2).wait()
+    for c in local(0, 1) + local(3, 0):
+        c.wait()
+    for t in range(4):
+        for slot, j, x0_only in sends[t]:
+            cs = remote(t, slot, j)
+            if x0_only:
+                @pl.when(on_x0)
+                def _(cs=cs):
+                    for c in cs:
+                        c.wait_send()
+
+                @pl.when(jnp.logical_not(on_x0))
+                def _(cs=cs):
+                    for c in cs:
+                        c.wait_recv()
+            else:
+                for c in cs:
+                    c.wait()
+    for c in wo_sends:
+        c.wait()
+
+
+def _qkv(x, g1, cos, sin, wq, wk, wv, wo, n):
     m, d = x.shape
     qw = wq.shape[1] // 4
     any_ = pl.BlockSpec(memory_space=pl.ANY)
     vm = pl.BlockSpec(memory_space=pltpu.VMEM)
+    kv = jax.ShapeDtypeStruct((n, 128), BF16)
     return pl.pallas_call(
         _qkv_body,
-        in_specs=[any_, vm, vm, vm, any_, any_, any_],
-        out_specs=[any_, any_, any_],
-        out_shape=[jax.ShapeDtypeStruct((n, qw), BF16), jax.ShapeDtypeStruct((n, 128), BF16), jax.ShapeDtypeStruct((n, 128), BF16)],
+        in_specs=[any_, vm, vm, vm, any_, any_, any_, any_],
+        out_specs=[any_] * 6,
+        out_shape=[jax.ShapeDtypeStruct((2, 2 * m, qw), BF16), kv, kv, kv, kv, jax.ShapeDtypeStruct(wo.shape, BF16)],
         scratch_shapes=[
             pltpu.VMEM((4, m // 4, d), BF16),
             pltpu.VMEM((m, d), BF16),
@@ -146,50 +209,85 @@
             pltpu.VMEM((4, m, 128), BF16),
             pltpu.SemaphoreType.DMA((4,)),
             pltpu.SemaphoreType.DMA((2, 3)),
-            pltpu.SemaphoreType.DMA((3, 2, 3)),
-            pltpu.SemaphoreType.DMA((3, 2, 3)),
-            pltpu.SemaphoreType.DMA((2, 3)),
+            pltpu.SemaphoreType.DMA((2, 4, 2)),
+            pltpu.SemaphoreType.DMA((2, 4, 2)),
+            pltpu.SemaphoreType.DMA((2, 2)),
+            pltpu.SemaphoreType.DMA((4,)),
+            pltpu.SemaphoreType.DMA((2,)),
+            pltpu.SemaphoreType.DMA((4,)),
+            pltpu.SemaphoreType.DMA((4,)),
         ],
         compiler_params=pltpu.CompilerParams(collective_id=1, has_side_effects=True, vmem_limit_bytes=56 * 2**20),
         cost_estimate=pl.CostEstimate(flops=2 * m * d * (4 * qw + 1024), bytes_accessed=80 * 2**20, transcendentals=0),
         name="qkv_exchange",
-    )(x, g1.reshape(1, -1), cos, sin, wq, wk, wv)
-
-
-def _attn_body(q_ref, k_ref, v_ref, own_hbm, oth_hbm, vt, acc, ms, ls, ob, ssem, rsem, lsem):
+    )(x, g1.reshape(1, -1), cos, sin, wq, wk, wv, wo)
+
+
+def _attn_body(q_ref, k0_hbm, v0_hbm, k1_hbm, v1_hbm, wo_hbm, woi_hbm, own_hbm, oth_hbm, wo_dst,
+               kb, vb, vt, acc, ms, ls, ob, kvsem, ssem, rsem0, rsem1, lsem, wsem, wrsem):
     rep, tp, s = lax.axis_index("rep"), lax.axis_index("tp"), lax.axis_index("sp")
     step = pl.program_id(0)
-    i = (step % 2) * 4 + step // 2
-    nh = q_ref.shape[1] // 128
     order = _sp_order(s)
+    far, diag, mate = order[:3]
+    nh = q_ref.shape[2] // 128
+    m = q_ref.shape[1] * 2
+    xrow = s // 2 * (2 * m)
+    qr = wo_hbm.shape[0] // 4
+    grp, r = step % 2, step // 2
+    nk = kb.shape[1]
+
+    wo_y = [_wo_y(tp, s, rep, wo_hbm, wo_dst, wsem.at[0, k], wrsem.at[0, k], k, WOP) for k in range(WOY, 4)]
+
+    def wo_piece(kind, k):
+        quarter = far if kind == 3 else s
+        r0 = pl.multiple_of(quarter * qr + k * WOP, 128)
+        return pltpu.make_async_remote_copy(src_ref=wo_dst.at[pl.ds(r0, WOP), :], dst_ref=wo_dst.at[pl.ds(r0, WOP), :],
+                                            send_sem=wsem.at[kind, k], recv_sem=wrsem.at[kind, k],
+                                            device_id=(rep, tp, far if kind == 1 else mate), device_id_type=MESH)
+
+    def kv_copies(g):
+        return [pltpu.make_async_copy((k0_hbm, k1_hbm)[g], kb.at[g], kvsem.at[g, 0]),
+                pltpu.make_async_copy((v0_hbm, v1_hbm)[g], vb.at[g], kvsem.at[g, 1])]
 
     @pl.when(step == 0)
     def _():
-        _barrier([(rep, tp, j) for j in order[:3]] + [(rep, 1 - tp, j) for j in range(4)])
-
-        @pl.loop(0, k_ref.shape[0] // 512)
-        def _(j):
-            r0 = pl.multiple_of(j * 512, 512)
-            vt[:, pl.ds(r0, 512)] = v_ref[pl.ds(r0, 512), :].T
+        for g in range(2):
+            for c in kv_copies(g):
+                c.start()
+        _barrier([(rep, tp, far), (rep, tp, mate), (rep, 1 - tp, s), (rep, 1 - tp, mate)])
+        for c in wo_y:
+            c.start()
+        for k in range(WOY):
+            wo_piece(1, k).start()
+            wo_piece(2, k).start()
+        for g in range(2):
+            for c in kv_copies(g):
+                c.wait()
+
+            @pl.loop(0, nk // 512)
+            def _(j, g=g):
+                r0 = pl.multiple_of(j * 512, 512)
+                vt[g, :, pl.ds(r0, 512)] = vb[g, pl.ds(r0, 512), :].T
 
     ms[...] = jnp.full_like(ms, NEG)
     ls[...] = jnp.zeros_like(ls)
     acc[...] = jnp.zeros_like(acc)
+    start = xrow + r * BQ
 
     def blk(k0, n, masked):
         k0 = pl.multiple_of(k0, BQ)
-        kb = k_ref[pl.ds(k0, n), :]
-        vb = vt[:, pl.ds(k0, n)]
+        kk_ = kb[grp, pl.ds(k0, n), :]
+        vv_ = vt[grp, :, pl.ds(k0, n)]
 
         def scores(h):
-            return lax.dot_general(kb, q_ref[:, h * 128:(h + 1) * 128], (((1,), (1,)), ((), ())), preferred_element_type=F32)
+            return lax.dot_general(kk_, q_ref[0, :, h * 128:(h + 1) * 128], (((1,), (1,)), ((), ())), preferred_element_type=F32)
 
         sc = scores(0)
         for h in range(nh):
             nxt = scores(h + 1) if h < nh - 1 else None
             if masked:
                 kk = lax.broadcasted_iota(jnp.int32, (n, BQ), 0)
-                qq = lax.broadcasted_iota(jnp.int32, (n, BQ), 1) + (i * BQ - k0)
+                qq = lax.broadcasted_iota(jnp.int32, (n, BQ), 1)
                 sc = jnp.where(qq >= kk, sc, NEG)
             m0 = ms[h:h + 1, :]
             m1 = jnp.maximum(m0, jnp.max(sc, axis=0, keepdims=True))
@@ -197,10 +295,8 @@
             a = jnp.exp2((m0 - m1) * SCALE_LOG2E)
             ms[h:h + 1, :] = m1
             ls[h:h + 1, :] = ls[h:h + 1, :] * a + jnp.sum(p, axis=0, keepdims=True)
-            acc[h] = acc[h] * a + jnp.dot(vb, p.astype(BF16), preferred_element_type=F32)
+            acc[h] = acc[h] * a + jnp.dot(vv_, p.astype(BF16), preferred_element_type=F32)
             sc = nxt
-
-    start = i * BQ
 
     @pl.loop(0, start // BK)
     def _(j):
@@ -215,35 +311,36 @@
         o = acc[h] * (1.0 / ls[h:h + 1, :])
         ob[step, :, h * 128:(h + 1) * 128] = o.T.astype(BF16)
 
-    w = q_ref.shape[1]
-
-    def dst(ref, slot, src_s):
-        return ref.at[slot, :, pl.ds(pl.multiple_of(src_s * w, 128), w)]
-
-    def to_own(step):
-        b = (step % 2) * 4 + step // 2
-        d, half = b // 2, b % 2
+    w = q_ref.shape[2]
+
+    def dst(ref, slot, src_s, g):
+        return ref.at[slot, :, pl.ds(pl.multiple_of((src_s + 2 * g) % 4 * w, 128), w)]
+
+    def place(t):
+        rr = t // 2
+        return t % 2, s // 2 * 2 + rr // 2, rr % 2
+
+    def to_own(t):
+        g, d, half = place(t)
         slot = (half + tp + 1) % 2
-        return d, slot, pltpu.make_async_remote_copy(
-            src_ref=ob.at[step], dst_ref=dst(own_hbm, slot, s), send_sem=ssem.at[0, step], recv_sem=rsem.at[0, s, slot],
-            device_id=(rep, tp, d), device_id_type=MESH)
-
-    def to_local(step):
-        b = (step % 2) * 4 + step // 2
-        half = b % 2
+        return pltpu.make_async_remote_copy(
+            src_ref=ob.at[t], dst_ref=dst(own_hbm, slot, s, g), send_sem=ssem.at[0, t], recv_sem=rsem0.at[g, slot],
+            device_id=(rep, tp, mate), device_id_type=MESH)
+
+    def to_local(t):
+        g, d, half = place(t)
         slot = (half + tp + 1) % 2
-        return pltpu.make_async_copy(ob.at[step], dst(own_hbm, slot, s), lsem.at[half])
-
-    def to_oth(step):
-        b = (step % 2) * 4 + step // 2
-        d, half = b // 2, b % 2
-        slot = (half + 1 - tp + 1) % 2
+        return pltpu.make_async_copy(ob.at[t], dst(own_hbm, slot, s, g), lsem.at[g, half])
+
+    def to_oth(t):
+        g, d, half = place(t)
+        slot = (half + tp) % 2
         return pltpu.make_async_remote_copy(
-            src_ref=ob.at[step], dst_ref=dst(oth_hbm, slot, s), send_sem=ssem.at[1, step], recv_sem=rsem.at[1, s, slot],
+            src_ref=ob.at[t], dst_ref=dst(oth_hbm, slot, s, g), send_sem=ssem.at[1, t], recv_sem=rsem1.at[s % 2, g, slot],
             device_id=(rep, 1 - tp, d), device_id_type=MESH)
 
     to_oth(step).start()
-    mine = i // 2 == s
+    mine = place(step)[1] == s
 
     @pl.when(mine)
     def _():
@@ -251,64 +348,90 @@
 
     @pl.when(jnp.logical_not(mine))
     def _():
-        to_own(step)[2].start()
+        to_own(step).start()
+
+    @pl.when(step == 2)
+    def _():
+        for i, c in enumerate(wo_y):
+            c.wait_recv()
+            wo_piece(1, WOY + i).start()
+            wo_piece(2, WOY + i).start()
+
+    for k in range(3):
+        @pl.when(step == 3 + k)
+        def _(k=k):
+            wo_piece(1, k).wait_recv()
+            wo_piece(3, k).start()
 
     @pl.when(step == pl.num_programs(0) - 1)
     def _():
+        wo_piece(1, 3).wait_recv()
+        wo_piece(3, 3).start()
+
         @pl.loop(0, 8)
         def _(t):
             to_oth(t).wait_send()
-            b = (t % 2) * 4 + t // 2
-
-            @pl.when(b // 2 == s)
+
+            @pl.when(place(t)[1] == s)
             def _():
                 to_local(t).wait()
 
-            @pl.when(b // 2 != s)
+            @pl.when(place(t)[1] != s)
             def _():
-                to_own(t)[2].wait_send()
-
-        @pl.loop(0, 4)
-        def _(j):
-            @pl.loop(0, 2)
-            def _(slot):
+                to_own(t).wait_send()
+
+        for g in range(2):
+            for slot in range(2):
                 pltpu.make_async_remote_copy(
-                    src_ref=ob.at[0], dst_ref=dst(oth_hbm, slot, j), send_sem=ssem.at[1, 0], recv_sem=rsem.at[1, j, slot],
-                    device_id=(rep, 1 - tp, j), device_id_type=MESH).wait_recv()
-
-                @pl.when(j != s)
-                def _():
+                    src_ref=ob.at[0], dst_ref=dst(own_hbm, slot, mate, g), send_sem=ssem.at[0, 0], recv_sem=rsem0.at[g, slot],
+                    device_id=(rep, tp, mate), device_id_type=MESH).wait_recv()
+                for core in range(2):
+                    src_s = s // 2 * 2 + core
                     pltpu.make_async_remote_copy(
-                        src_ref=ob.at[0], dst_ref=dst(own_hbm, slot, j), send_sem=ssem.at[0, 0], recv_sem=rsem.at[0, j, slot],
-                        device_id=(rep, tp, j), device_id_type=MESH).wait_recv()
-
-
-def _attention(q, k, v):
-    n, w = q.shape
+                        src_ref=ob.at[0], dst_ref=dst(oth_hbm, slot, src_s, g), send_sem=ssem.at[1, 0], recv_sem=rsem1.at[core, g, slot],
+                        device_id=(rep, 1 - tp, src_s), device_id_type=MESH).wait_recv()
+        for c in wo_y:
+            c.wait_send()
+        for k in range(4):
+            wo_piece(1, k).wait_send()
+            wo_piece(2, k).wait()
+            wo_piece(3, k).wait()
+
+
+def _attention(q, k0, v0, k1, v1, wo, wo_oth):
+    n = k0.shape[0]
+    _, m2, w = q.shape
     nh = w // 128
+    steps = 2 * m2 // BQ
     any_ = pl.BlockSpec(memory_space=pl.ANY)
-    full = pl.BlockSpec((n, 128), lambda t: (0, 0))
     shape = jax.ShapeDtypeStruct((2, BQ, 4 * w), BF16)
     return pl.pallas_call(
         _attn_body,
-        grid=(n // BQ,),
-        in_specs=[pl.BlockSpec((BQ, w), lambda t: ((t % 2) * 4 + t // 2, 0)), full, full],
-        out_specs=[any_, any_],
-        out_shape=[shape, shape],
+        grid=(steps,),
+        in_specs=[pl.BlockSpec((1, BQ, w), lambda t: (t % 2, t // 2, 0))] + [any_] * 6,
+        out_specs=[any_] * 3,
+        out_shape=[shape, shape, jax.ShapeDtypeStruct(wo.shape, BF16)],
+        input_output_aliases={6: 2},
         scratch_shapes=[
-            pltpu.VMEM((128, n), BF16),
+            pltpu.VMEM((2, n, 128), BF16),
+            pltpu.VMEM((2, n, 128), BF16),
+            pltpu.VMEM((2, 128, n), BF16),
             pltpu.VMEM((nh, 128, BQ), F32),
             pltpu.VMEM((8, BQ), F32),
             pltpu.VMEM((8, BQ), F32),
-            pltpu.VMEM((n // BQ, BQ, w), BF16),
+            pltpu.VMEM((steps, BQ, w), BF16),
+            pltpu.SemaphoreType.DMA((2, 2)),
             pltpu.SemaphoreType.DMA((2, 8)),
-            pltpu.SemaphoreType.DMA((2, 4, 2)),
-            pltpu.SemaphoreType.DMA((2,)),
+            pltpu.SemaphoreType.DMA((2, 2)),
+            pltpu.SemaphoreType.DMA((2, 2, 2)),
+            pltpu.SemaphoreType.DMA((2, 2)),
+            pltpu.SemaphoreType.DMA((4, 4)),
+            pltpu.SemaphoreType.DMA((4, 4)),
         ],
         compiler_params=pltpu.CompilerParams(collective_id=2, has_side_effects=True, vmem_limit_bytes=56 * 2**20),
         cost_estimate=pl.CostEstimate(flops=2 * n * n * w * 2, bytes_accessed=16 * 2**20, transcendentals=0),
         name="attention_exchange",
-    )(q, k, v)
+    )(q, k0, v0, k1, v1, wo, wo_oth)
 
 
 NWO, NHID, NW2 = 8, 28, 16
@@ -317,26 +440,21 @@
 MB = 256
 
 
-def _mlp_body(chunks, own_hbm, oth_hbm, x_hbm, wo_hbm, p0, p1, p2, p3, g_ref, w1_hbm, w3_hbm, w2_hbm, y_hbm,
+def _mlp_body(chunks, own_hbm, oth_hbm, x_hbm, wo_hbm, wo_oth_hbm, g_ref, w1_hbm, w3_hbm, w2_hbm, y_hbm,
               wb, abuf, xbuf, hid, pbuf, rbuf, ybuf, wsem, asem, ssem, rsem, ysem, yrsem, ylsem):
     rep, tp, s = lax.axis_index("rep"), lax.axis_index("tp"), lax.axis_index("sp")
     hr = wo_hbm.shape[0]
-    qr = hr // 4
     hm = x_hbm.shape[0] // 2
     kh = w2_hbm.shape[0] // 2
     total = UNITS * len(chunks)
-    s1 = s + 1 - 2 * (s % 2)
-    quarters = [(p0, s), (p1, (s + 2) % 4), (p2, s1), (p3, (s1 + 2) % 4)]
     partner = (rep, 1 - tp, s)
 
     def col(j, w):
         return pl.ds(pl.multiple_of(j * w, w), w)
 
     def wo_copies(j, sl):
-        cs = [pltpu.make_async_copy(wo_hbm.at[:, col(j, 512)], wb.at[sl, pl.ds(0, hr), :], wsem.at[sl, 0])]
-        for n, (p, r) in enumerate(quarters):
-            cs.append(pltpu.make_async_copy(p.at[:, col(j, 512)], wb.at[sl, pl.ds(pl.multiple_of(hr + r * qr, qr), qr), :], wsem.at[sl, n + 1]))
-        return cs
+        return [pltpu.make_async_copy(wo_hbm.at[:, col(j, 512)], wb.at[sl, pl.ds(0, hr), :], wsem.at[sl, 0]),
+                pltpu.make_async_copy(wo_oth_hbm.at[:, col(j, 512)], wb.at[sl, pl.ds(hr, hr), :], wsem.at[sl, 1])]
 
     def hid_copies(j, sl):
         return [pltpu.make_async_copy(w1_hbm.at[:, col(j, 256)], wb.at[sl, :, pl.ds(0, 256)], wsem.at[sl, 0]),
@@ -483,7 +601,7 @@
         yrecv(j).wait_recv()
 
 
-def _mlp(own, oth, x, wo, pieces, g2, w1, w3, w2):
+def _mlp(own, oth, x, wo, wo_oth, g2, w1, w3, w2):
     m, d = x.shape
     hm = m // 2
     chunks = ((0, 0, 256), (0, 256, 256), (1, 0, 512))
@@ -492,7 +610,7 @@
     nt = NW2 // 2
     return pl.pallas_call(
         functools.partial(_mlp_body, chunks),
-        in_specs=[any_] * 8 + [vm] + [any_] * 3,
+        in_specs=[any_] * 5 + [vm] + [any_] * 3,
         out_specs=any_,
         out_shape=jax.ShapeDtypeStruct((m, d), BF16),
         scratch_shapes=[
@@ -503,7 +621,7 @@
             pltpu.VMEM((nt + 1, hm, 512), F32),
             pltpu.VMEM((nt, hm, 512), F32),
             pltpu.VMEM((nt, hm, 512), BF16),
-            pltpu.SemaphoreType.DMA((NBUF, 5)),
+            pltpu.SemaphoreType.DMA((NBUF, 2)),
             pltpu.SemaphoreType.DMA((3,)),
             pltpu.SemaphoreType.DMA((2, nt)),
             pltpu.SemaphoreType.DMA((2, nt)),
@@ -514,7 +632,7 @@
         compiler_params=pltpu.CompilerParams(collective_id=3, has_side_effects=True, vmem_limit_bytes=67043328),
         cost_estimate=pl.CostEstimate(flops=2 * m * d * (d + 3 * w1.shape[1]), bytes_accessed=640 * 2**20, transcendentals=0),
         name="mlp_sum",
-    )(own, oth, x, wo, *pieces, g2.reshape(1, -1), w1, w3, w2)
+    )(own, oth, x, wo, wo_oth, g2.reshape(1, -1), w1, w3, w2)
 
 
 def solution(mesh):
@@ -522,24 +640,14 @@
     col = P(None, "tp")
     row = P("tp", None)
     cache = P("rep", ("tp", "sp"), None)
-    swap = [(0, 1), (1, 0)]
 
     def local(x, pos, g1, g2, wq, wk, wv, wo, w1, w3, w2):
         m, d = x.shape
         n = m * mesh.shape["sp"]
-        s = lax.axis_index("sp")
-        qr = wo.shape[0] // 4
-        piece = lax.ppermute(lax.dynamic_slice(wo, (s * qr, 0), (qr, d)), "tp", swap)
         cos, sin = _tables(pos)
-        q, k, v = _qkv(x, g1, cos, sin, wq, wk, wv, n)
-        piece, q = lax.optimization_barrier((piece, q))
-        far = lax.ppermute(piece, "sp", [(0, 2), (2, 0), (1, 3), (3, 1)])
-        own, oth = _attention(q, k, v)
-        far, own, oth = lax.optimization_barrier((far, own, oth))
-        cross = [(0, 1), (1, 0), (2, 3), (3, 2)]
-        near = lax.ppermute(piece, "sp", cross)
-        near2 = lax.ppermute(far, "sp", cross)
-        y = _mlp(own, oth, x, wo, (piece, far, near, near2), g2, w1, w3, w2)
+        q, k, v, k1, v1, wo_oth = _qkv(x, g1, cos, sin, wq, wk, wv, wo, n)
+        own, oth, wo_oth = _attention(q, k, v, k1, v1, wo, wo_oth)
+        y = _mlp(own, oth, x, wo, wo_oth, g2, w1, w3, w2)
         return y, k.reshape(n, 1, 128), v.reshape(n, 1, 128)
 
     return jax.shard_map(

time: 629 us -> 534 us (0.85)
  Pallas kernels: 590 us -> 519 us
  waiting for transfers between devices: 12.3 us -> 0 us
  local copies, waits for them, and re-layouts: 16.6 us -> 9.98 us
    pallas_call x3, Pallas kernels: 590 us -> 519 us  [the longest x1 329 us: _mlp(): pl.pallas_call(functools.partial(_mlp_body, chunks), in_specs=[any_] * 5...]
    ppermute x4 -> x0, waiting for transfers between devices: 12.3 us -> none  [the longest x1 6.78 us: local(): near2 = lax.ppermute(far, 'sp', cross)]
    unnamed x13 -> x7, local copies, waits for them, and re-layouts: 14 us -> 9.98 us
  transfers between devices with their start and end apart: 4 -> 0, of which waited for: 2 -> 0; matrix products, arithmetic and copies ran while one was open for 1% -> 0% of each run, Pallas kernels for 42% -> 0%
where the time goes in v2:
time: 534 us; the launch traced here: 533 us
  Pallas kernels  519 us (97%)
  local copies, waits for them, and re-layouts  9.98 us (2%)
    pallas_call x1, Pallas kernels, _mlp(): pl.pallas_call(functools.partial(_mlp_body, chunks), in_specs=[any_] * 5...  329 us
    pallas_call x1, Pallas kernels, _attention(): pl.pallas_call(_attn_body, grid=(steps,), in_specs=[pl.BlockSpec((1, BQ,...  115 us
    pallas_call x1, Pallas kernels, _qkv(): pl.pallas_call(_qkv_body, in_specs=[any_, vm, vm, vm, any_, any_, any_, a...  75 us

profile of v2, /device:TPU:0, one launch (start us, length us, event | category | flops | bytes accessed | tf_op | source)
XLA Modules:
  0.0 533.4 jit_solution(2948050750604554785)
XLA Ops:
  0.6 0.7 convert_element_type.3
  1.3 1.9 fusion
  3.2 1.3 pad_maximum_fusion
  4.6 75.0 %qkv_exchange.1 = (bf16[2,2048,512]{2,1,0:T(8,128)(2,1)}, bf16[4096,128]{1,0:T(8,128)(2,1)}, bf16[4096,128]{1,0:T(8,128)(2,1)}, bf16[4096,128]{1,0:T(8,128)(2,1)...) custom-call(bf16[1024,4096]{1,0:T(8,128)(2,1)} %x_hbm.3, f32[1,4096]{1,0:T(1,128)} %bitcast.6, ...), custom_call_target="tpu_custom_call" | custom-call | flops 25769803776 | bytes 83886080 | tf_op jit(solution)/shard_map/qkv_exchange/pallas_call | solution.py:197
  79.6 115.3 %attention_exchange.1 = (bf16[2,512,2048]{2,1,0:T(8,128)(2,1)}, bf16[2,512,2048]{2,1,0:T(8,128)(2,1)}, bf16[2048,4096]{1,0:T(8,128)(2,1)}) custom-call(bf16[2,2048,512]{2,1,0:T(8,128)(2,1)} %get-tuple-element.12.q_ref, bf16[4096,128]{1,0:T(8,128)(2,1)} %get-tuple-element.13.k0_hbm, ...), custom_call_target="tpu_custom_call", output_to_operand_aliasing={{2}: (6, {})} | custom-call | flops 34359738368 | bytes 16777216 | tf_op jit(solution)/shard_map/attention_exchange/pallas_call | solution.py:408
  194.8 328.6 %mlp_sum.1 = bf16[1024,4096]{1,0:T(8,128)(2,1)} custom-call(bf16[2,512,2048]{2,1,0:T(8,128)(2,1)} %get-tuple-element.18.own_hbm, bf16[2,512,2048]{2,1,0:T(8,128)(2,1)} %get-tuple-element.19.oth_hbm, bf16[1024,4096]{1,0:T(8,128)(2,1)} %x_hbm.3, bf16[2048,4096]{1,0:T(8,128)(2,1)} %wo_hbm.5, bf16[2048,4096]{1,0:T(8,128)(2,1)} %get-tuple-element.20.wo_oth_hbm, ...), custom_call_target="tpu_custom_call" | custom-call | flops 214748364800 | bytes 671088640 | tf_op jit(solution)/shard_map/mlp_sum/pallas_call | solution.py:611
  523.4 0.0 copy-start.1
  523.4 0.0 copy-start
  523.4 8.0 %copy.19 = bf16[1024,4096]{1,0:T(8,128)(2,1)} copy(bf16[1024,4096]{1,0:T(8,128)(2,1)} %mlp_sum.1) | data formatting | bytes 16777216
  531.5 0.0 copy-done.1
  531.5 1.0 copy.20
  532.4 0.0 copy-done
  532.4 1.0 copy.21
  (1 shorter events, 0.0 us)
Async XLA Ops:
  523.4 8.1 %copy-start.1 = (bf16[4096,128]{1,0:T(8,128)(2,1)S(1)}, bf16[4096,128]{1,0:T(8,128)(2,1)}, u32[]{:S(2)}) copy-start(bf16[4096,128]{1,0:T(8,128)(2,1)} %get-tuple-element.13.k0_hbm) | copy-start | bytes 3145732
  523.4 9.0 %copy-start = (bf16[4096,128]{1,0:T(8,128)(2,1)S(1)}, bf16[4096,128]{1,0:T(8,128)(2,1)}, u32[]{:S(2)}) copy-start(bf16[4096,128]{1,0:T(8,128)(2,1)} %get-tuple-element.14.v0_hbm) | copy-start | bytes 3145732

commit v3 on v2

--- a/solution.py
+++ b/solution.py
@@ -15,7 +15,7 @@
 BQ = 512
 BK = 1024
 WOP = 128
-WOY = 3
+WOY = 2
 MESH = pl.DeviceIdType.MESH
 F32 = jnp.float32
 BF16 = jnp.bfloat16
@@ -141,14 +141,15 @@
             for c in kvcopies(t + 2):
                 c.start()
 
-    qrow = pl.ds(pl.multiple_of(s % 2 * m, 128), m)
-
-    def qremote(t):
-        return pltpu.make_async_remote_copy(src_ref=qo.at[t], dst_ref=q_hbm.at[t % 2, qrow, :], send_sem=qsem.at[t], recv_sem=qrsem.at[t],
-                                            device_id=(rep, tp, mate), device_id_type=MESH)
-
-    def qlocal(t):
-        return pltpu.make_async_copy(qo.at[t], q_hbm.at[t % 2, qrow, :], qsem.at[t])
+    hm = m // 2
+
+    def qmove(t, h):
+        src = qo.at[t, pl.ds(h * hm, hm), :]
+        to = q_hbm.at[t % 2, pl.ds(pl.multiple_of(((h + tp) % 2 * 2 + s % 2) * hm, 128), hm), :]
+        if t < 2:
+            return pltpu.make_async_remote_copy(src_ref=src, dst_ref=to, send_sem=qsem.at[t, h], recv_sem=qrsem.at[t, h],
+                                                device_id=(rep, tp, mate), device_id_type=MESH)
+        return pltpu.make_async_copy(src, to, qsem.at[t, h])
 
     for t in range(4):
         qcopy(t).wait()
@@ -159,13 +160,14 @@
             qq = jnp.dot(u[pl.ds(r0, 256), :], wq[t % 2], preferred_element_type=F32)
             for n in range(qw // 128):
                 qo[t, pl.ds(r0, 256), n * 128:(n + 1) * 128] = rope(qq[:, n * 128:(n + 1) * 128], r0).astype(BF16)
-        (qremote(t) if t < 2 else qlocal(t)).start()
+        for h in range(2):
+            qmove(t, h).start()
         if t < 2:
             qcopy(t + 2).start()
 
-    for t in range(2):
-        qremote(t).wait()
-        qlocal(t + 2).wait()
+    for t in range(4):
+        for h in range(2):
+            qmove(t, h).wait()
     for c in local(0, 1) + local(3, 0):
         c.wait()
     for t in range(4):
@@ -212,8 +214,8 @@
             pltpu.SemaphoreType.DMA((2, 4, 2)),
             pltpu.SemaphoreType.DMA((2, 4, 2)),
             pltpu.SemaphoreType.DMA((2, 2)),
-            pltpu.SemaphoreType.DMA((4,)),
-            pltpu.SemaphoreType.DMA((2,)),
+            pltpu.SemaphoreType.DMA((4, 2)),
+            pltpu.SemaphoreType.DMA((2, 2)),
             pltpu.SemaphoreType.DMA((4,)),
             pltpu.SemaphoreType.DMA((4,)),
         ],
@@ -223,8 +225,13 @@
     )(x, g1.reshape(1, -1), cos, sin, wq, wk, wv, wo)
 
 
-def _attn_body(q_ref, k0_hbm, v0_hbm, k1_hbm, v1_hbm, wo_hbm, woi_hbm, own_hbm, oth_hbm, wo_dst,
-               kb, vb, vt, acc, ms, ls, ob, kvsem, ssem, rsem0, rsem1, lsem, wsem, wrsem):
+def _place(t, tp):
+    i = t // 2
+    return t % 2, i % 2, (tp + i // 2) % 2
+
+
+def _attn_body(q_ref, k0_hbm, v0_hbm, k1_hbm, v1_hbm, wo_hbm, woi_hbm, own_hbm, oth_hbm, wo_dst, late_hbm,
+               kb, vb, vt, acc, ms, ls, ob, kvsem, ssem, rsem0, rsem1, lsem, lasem, wsem, wrsem):
     rep, tp, s = lax.axis_index("rep"), lax.axis_index("tp"), lax.axis_index("sp")
     step = pl.program_id(0)
     order = _sp_order(s)
@@ -233,7 +240,8 @@
     m = q_ref.shape[1] * 2
     xrow = s // 2 * (2 * m)
     qr = wo_hbm.shape[0] // 4
-    grp, r = step % 2, step // 2
+    grp, cc, half = _place(step, tp)
+    r = 2 * cc + half
     nk = kb.shape[1]
 
     wo_y = [_wo_y(tp, s, rep, wo_hbm, wo_dst, wsem.at[0, k], wrsem.at[0, k], k, WOP) for k in range(WOY, 4)]
@@ -313,52 +321,62 @@
 
     w = q_ref.shape[2]
 
+    def cols(src_s, g):
+        return pl.ds(pl.multiple_of((src_s + 2 * g) % 4 * w, 128), w)
+
     def dst(ref, slot, src_s, g):
-        return ref.at[slot, :, pl.ds(pl.multiple_of((src_s + 2 * g) % 4 * w, 128), w)]
-
-    def place(t):
-        rr = t // 2
-        return t % 2, s // 2 * 2 + rr // 2, rr % 2
+        return ref.at[slot, :, cols(src_s, g)]
 
     def to_own(t):
-        g, d, half = place(t)
+        g, _, half = _place(t, tp)
         slot = (half + tp + 1) % 2
         return pltpu.make_async_remote_copy(
             src_ref=ob.at[t], dst_ref=dst(own_hbm, slot, s, g), send_sem=ssem.at[0, t], recv_sem=rsem0.at[g, slot],
             device_id=(rep, tp, mate), device_id_type=MESH)
 
     def to_local(t):
-        g, d, half = place(t)
+        g, _, half = _place(t, tp)
         slot = (half + tp + 1) % 2
         return pltpu.make_async_copy(ob.at[t], dst(own_hbm, slot, s, g), lsem.at[g, half])
 
     def to_oth(t):
-        g, d, half = place(t)
-        slot = (half + tp) % 2
+        g, cc, _ = _place(t, tp)
         return pltpu.make_async_remote_copy(
-            src_ref=ob.at[t], dst_ref=dst(oth_hbm, slot, s, g), send_sem=ssem.at[1, t], recv_sem=rsem1.at[s % 2, g, slot],
-            device_id=(rep, 1 - tp, d), device_id_type=MESH)
-
-    to_oth(step).start()
-    mine = place(step)[1] == s
-
-    @pl.when(mine)
+            src_ref=ob.at[t], dst_ref=oth_hbm.at[:, cols(s, g)], send_sem=ssem.at[1, t], recv_sem=rsem1.at[s % 2, g],
+            device_id=(rep, 1 - tp, s // 2 * 2 + cc), device_id_type=MESH)
+
+    def to_late(t):
+        g, cc, _ = _place(t, tp)
+        return pltpu.make_async_copy(ob.at[t], late_hbm.at[g, cc], lasem.at[g, cc])
+
+    @pl.when(step < 4)
+    def _():
+        to_oth(step).start()
+
+    @pl.when(step >= 4)
+    def _():
+        to_late(step).start()
+
+    def mine(t):
+        return _place(t, tp)[1] == s % 2
+
+    @pl.when(mine(step))
     def _():
         to_local(step).start()
 
-    @pl.when(jnp.logical_not(mine))
+    @pl.when(jnp.logical_not(mine(step)))
     def _():
         to_own(step).start()
 
-    @pl.when(step == 2)
-    def _():
-        for i, c in enumerate(wo_y):
-            c.wait_recv()
-            wo_piece(1, WOY + i).start()
-            wo_piece(2, WOY + i).start()
+    for k in range(WOY, 4):
+        @pl.when(step == 2 * (k - WOY) + 2)
+        def _(k=k):
+            wo_y[k - WOY].wait_recv()
+            wo_piece(1, k).start()
+            wo_piece(2, k).start()
 
     for k in range(3):
-        @pl.when(step == 3 + k)
+        @pl.when(step == 2 * k + 2)
         def _(k=k):
             wo_piece(1, k).wait_recv()
             wo_piece(3, k).start()
@@ -368,15 +386,18 @@
         wo_piece(1, 3).wait_recv()
         wo_piece(3, 3).start()
 
+        @pl.loop(0, 4)
+        def _(t):
+            to_oth(t).wait_send()
+            to_late(t + 4).wait()
+
         @pl.loop(0, 8)
         def _(t):
-            to_oth(t).wait_send()
-
-            @pl.when(place(t)[1] == s)
+            @pl.when(mine(t))
             def _():
                 to_local(t).wait()
 
-            @pl.when(place(t)[1] != s)
+            @pl.when(jnp.logical_not(mine(t)))
             def _():
                 to_own(t).wait_send()
 
@@ -385,11 +406,11 @@
                 pltpu.make_async_remote_copy(
                     src_ref=ob.at[0], dst_ref=dst(own_hbm, slot, mate, g), send_sem=ssem.at[0, 0], recv_sem=rsem0.at[g, slot],
                     device_id=(rep, tp, mate), device_id_type=MESH).wait_recv()
-                for core in range(2):
-                    src_s = s // 2 * 2 + core
-                    pltpu.make_async_remote_copy(
-                        src_ref=ob.at[0], dst_ref=dst(oth_hbm, slot, src_s, g), send_sem=ssem.at[1, 0], recv_sem=rsem1.at[core, g, slot],
-                        device_id=(rep, 1 - tp, src_s), device_id_type=MESH).wait_recv()
+            for core in range(2):
+                src_s = s // 2 * 2 + core
+                pltpu.make_async_remote_copy(
+                    src_ref=ob.at[0], dst_ref=oth_hbm.at[:, cols(src_s, g)], send_sem=ssem.at[1, 0], recv_sem=rsem1.at[core, g],
+                    device_id=(rep, 1 - tp, src_s), device_id_type=MESH).wait_recv()
         for c in wo_y:
             c.wait_send()
         for k in range(4):
@@ -409,8 +430,9 @@
         _attn_body,
         grid=(steps,),
         in_specs=[pl.BlockSpec((1, BQ, w), lambda t: (t % 2, t // 2, 0))] + [any_] * 6,
-        out_specs=[any_] * 3,
-        out_shape=[shape, shape, jax.ShapeDtypeStruct(wo.shape, BF16)],
+        out_specs=[any_] * 4,
+        out_shape=[shape, jax.ShapeDtypeStruct((BQ, 4 * w), BF16), jax.ShapeDtypeStruct(wo.shape, BF16),
+                   jax.ShapeDtypeStruct((2, 2, BQ, w), BF16)],
         input_output_aliases={6: 2},
         scratch_shapes=[
             pltpu.VMEM((2, n, 128), BF16),
@@ -423,7 +445,8 @@
             pltpu.SemaphoreType.DMA((2, 2)),
             pltpu.SemaphoreType.DMA((2, 8)),
             pltpu.SemaphoreType.DMA((2, 2)),
-            pltpu.SemaphoreType.DMA((2, 2, 2)),
+            pltpu.SemaphoreType.DMA((2, 2)),
+            pltpu.SemaphoreType.DMA((2, 2)),
             pltpu.SemaphoreType.DMA((2, 2)),
             pltpu.SemaphoreType.DMA((4, 4)),
             pltpu.SemaphoreType.DMA((4, 4)),
@@ -440,8 +463,8 @@
 MB = 256
 
 
-def _mlp_body(chunks, own_hbm, oth_hbm, x_hbm, wo_hbm, wo_oth_hbm, g_ref, w1_hbm, w3_hbm, w2_hbm, y_hbm,
-              wb, abuf, xbuf, hid, pbuf, rbuf, ybuf, wsem, asem, ssem, rsem, ysem, yrsem, ylsem):
+def _mlp_body(chunks, own_hbm, oth_hbm, x_hbm, wo_hbm, wo_oth_hbm, g_ref, w1_hbm, w3_hbm, w2_hbm, late_hbm, y_hbm, olate_hbm,
+              wb, abuf, xbuf, hid, pbuf, rbuf, ybuf, wsem, asem, ssem, rsem, ysem, yrsem, ylsem, lasem, larsem):
     rep, tp, s = lax.axis_index("rep"), lax.axis_index("tp"), lax.axis_index("sp")
     hr = wo_hbm.shape[0]
     hm = x_hbm.shape[0] // 2
@@ -489,7 +512,7 @@
         rs = pl.ds(0, nr)
         return (pltpu.make_async_copy(x_hbm.at[pl.ds(pl.multiple_of(base, 128), nr), :], xbuf.at[rs, :], asem.at[0]),
                 [pltpu.make_async_copy(own_hbm.at[slot, pl.ds(r0, nr), :], abuf.at[rs, pl.ds(0, hr)], asem.at[1]),
-                 pltpu.make_async_copy(oth_hbm.at[slot, pl.ds(r0, nr), :], abuf.at[rs, pl.ds(hr, hr)], asem.at[2])])
+                 pltpu.make_async_copy((oth_hbm if slot == 0 else olate_hbm).at[pl.ds(r0, nr), :], abuf.at[rs, pl.ds(hr, hr)], asem.at[2])])
 
     for g in range(NBUF - 1):
         issue(g)
@@ -497,7 +520,19 @@
     xc.start()
     for c in ac:
         c.start()
-    _barrier([partner])
+    mate = s + 1 - 2 * (s % 2)
+    _barrier([partner, (rep, 1 - tp, mate)])
+    w = late_hbm.shape[3]
+
+    def late(g, cc, src_s):
+        return pltpu.make_async_remote_copy(
+            src_ref=late_hbm.at[g, cc], dst_ref=olate_hbm.at[:, pl.ds(pl.multiple_of((src_s + 2 * g) % 4 * w, 128), w)],
+            send_sem=lasem.at[g, cc], recv_sem=larsem.at[g, src_s % 2],
+            device_id=(rep, 1 - tp, s // 2 * 2 + cc), device_id_type=MESH)
+
+    for g in range(2):
+        for cc in range(2):
+            late(g, cc, s).start()
 
     def send(ci, j):
         slot, r0, nr = chunks[ci]
@@ -560,6 +595,10 @@
                 a = ab[:, :256]
                 hid[rs, col(j, 256)] = (a / (1.0 + jnp.exp(-a)) * ab[:, 256:]).astype(BF16)
 
+        if ci + 2 == len(chunks):
+            for g in range(2):
+                for core in range(2):
+                    late(g, core, s // 2 * 2 + core).wait_recv()
         if ci + 1 < len(chunks):
             for c in acts(ci + 1)[1]:
                 c.start()
@@ -592,6 +631,10 @@
                 ysend(j).start()
                 yown(j).start()
 
+    for g in range(2):
+        for cc in range(2):
+            late(g, cc, s).wait_send()
+
     @pl.loop(0, NW2 // 2)
     def _(j):
         for k in range(nsend):
@@ -601,7 +644,7 @@
         yrecv(j).wait_recv()
 
 
-def _mlp(own, oth, x, wo, wo_oth, g2, w1, w3, w2):
+def _mlp(own, oth, late, x, wo, wo_oth, g2, w1, w3, w2):
     m, d = x.shape
     hm = m // 2
     chunks = ((0, 0, 256), (0, 256, 256), (1, 0, 512))
@@ -610,9 +653,9 @@
     nt = NW2 // 2
     return pl.pallas_call(
         functools.partial(_mlp_body, chunks),
-        in_specs=[any_] * 5 + [vm] + [any_] * 3,
-        out_specs=any_,
-        out_shape=jax.ShapeDtypeStruct((m, d), BF16),
+        in_specs=[any_] * 5 + [vm] + [any_] * 4,
+        out_specs=[any_, any_],
+        out_shape=[jax.ShapeDtypeStruct((m, d), BF16), jax.ShapeDtypeStruct((hm, wo.shape[0]), BF16)],
         scratch_shapes=[
             pltpu.VMEM((NBUF, d, 512), BF16),
             pltpu.VMEM((hm, d), BF16),
@@ -628,11 +671,13 @@
             pltpu.SemaphoreType.DMA((nt,)),
             pltpu.SemaphoreType.DMA((nt,)),
             pltpu.SemaphoreType.DMA((nt,)),
+            pltpu.SemaphoreType.DMA((2, 2)),
+            pltpu.SemaphoreType.DMA((2, 2)),
         ],
         compiler_params=pltpu.CompilerParams(collective_id=3, has_side_effects=True, vmem_limit_bytes=67043328),
         cost_estimate=pl.CostEstimate(flops=2 * m * d * (d + 3 * w1.shape[1]), bytes_accessed=640 * 2**20, transcendentals=0),
         name="mlp_sum",
-    )(own, oth, x, wo, wo_oth, g2.reshape(1, -1), w1, w3, w2)
+    )(own, oth, x, wo, wo_oth, g2.reshape(1, -1), w1, w3, w2, late)[0]
 
 
 def solution(mesh):
@@ -646,8 +691,8 @@
         n = m * mesh.shape["sp"]
         cos, sin = _tables(pos)
         q, k, v, k1, v1, wo_oth = _qkv(x, g1, cos, sin, wq, wk, wv, wo, n)
-        own, oth, wo_oth = _attention(q, k, v, k1, v1, wo, wo_oth)
-        y = _mlp(own, oth, x, wo, wo_oth, g2, w1, w3, w2)
+        own, oth, wo_oth, late = _attention(q, k, v, k1, v1, wo, wo_oth)
+        y = _mlp(own, oth, late, x, wo, wo_oth, g2, w1, w3, w2)
         return y, k.reshape(n, 1, 128), v.reshape(n, 1, 128)
 
     return jax.shard_map(

time: 534 us -> 500 us (0.936)
  Pallas kernels: 519 us -> 485 us
    pallas_call x1, Pallas kernels: 75 us -> 58.1 us  [_qkv(): pl.pallas_call(_qkv_body, in_specs=[any_, vm, vm, vm, any_, any_, any_, a...]
    pallas_call x1, Pallas kernels: 115 us -> 99.8 us  [_attention(): pl.pallas_call(_attn_body, grid=(steps,), in_specs=[pl.BlockSpec((1, BQ,...]
where the time goes in v3:
time: 500 us
  Pallas kernels  485 us (97%)
  local copies, waits for them, and re-layouts  9.98 us (2%)
    pallas_call x1, Pallas kernels, _mlp(): pl.pallas_call(functools.partial(_mlp_body, chunks), in_specs=[any_] * 5...  327 us
    pallas_call x1, Pallas kernels, _attention(): pl.pallas_call(_attn_body, grid=(steps,), in_specs=[pl.BlockSpec((1, BQ,...  99.8 us
    pallas_call x1, Pallas kernels, _qkv(): pl.pallas_call(_qkv_body, in_specs=[any_, vm, vm, vm, any_, any_, any_, a...  58.1 us

profile of v3, /device:TPU:0, one launch (start us, length us, event | category | flops | bytes accessed | tf_op | source)
XLA Modules:
  0.0 499.8 jit_solution(11086566814042663629)
XLA Ops:
  0.6 0.7 convert_element_type.3
  1.3 1.9 fusion
  3.2 1.3 pad_maximum_fusion
  4.6 58.1 %qkv_exchange.1 = (bf16[2,2048,512]{2,1,0:T(8,128)(2,1)}, bf16[4096,128]{1,0:T(8,128)(2,1)}, bf16[4096,128]{1,0:T(8,128)(2,1)}, bf16[4096,128]{1,0:T(8,128)(2,1)...) custom-call(bf16[1024,4096]{1,0:T(8,128)(2,1)} %x_hbm.3, f32[1,4096]{1,0:T(1,128)} %bitcast.6, ...), custom_call_target="tpu_custom_call" | custom-call | flops 25769803776 | bytes 83886080 | tf_op jit(solution)/shard_map/qkv_exchange/pallas_call | solution.py:199
  62.7 99.8 %attention_exchange.1 = (bf16[2,512,2048]{2,1,0:T(8,128)(2,1)}, bf16[512,2048]{1,0:T(8,128)(2,1)}, bf16[2048,4096]{1,0:T(8,128)(2,1)}, bf16[2,2,512,512]{3,2,1,0:T(8,128)(2,1)}) custom-call(bf16[2,2048,512]{2,1,0:T(8,128)(2,1)} %get-tuple-element.14.q_ref, bf16[4096,128]{1,0:T(8,128)(2,1)} %get-tuple-element.15.k0_hbm, ...), custom_call_target="tpu_custom_call", output_to_operand_aliasing={{2}: (6, {})} | custom-call | flops 34359738368 | bytes 16777216 | tf_op jit(solution)/shard_map/attention_exchange/pallas_call | solution.py:429
  162.6 327.2 %mlp_sum.1 = (bf16[1024,4096]{1,0:T(8,128)(2,1)}, bf16[512,2048]{1,0:T(8,128)(2,1)}) custom-call(bf16[2,512,2048]{2,1,0:T(8,128)(2,1)} %get-tuple-element.20.own_hbm, bf16[512,2048]{1,0:T(8,128)(2,1)} %get-tuple-element.21.oth_hbm, bf16[1024,4096]{1,0:T(8,128)(2,1)} %x_hbm.3, bf16[2048,4096]{1,0:T(8,128)(2,1)} %wo_hbm.5, ...), custom_call_target="tpu_custom_call" | custom-call | flops 214748364800 | bytes 671088640 | tf_op jit(solution)/shard_map/mlp_sum/pallas_call | solution.py:654
  489.8 0.0 copy-start.1
  489.8 0.0 copy-start
  489.8 8.0 %copy.19 = bf16[1024,4096]{1,0:T(8,128)(2,1)} copy(bf16[1024,4096]{1,0:T(8,128)(2,1)} %get-tuple-element.33) | data formatting | bytes 16777216
  497.9 0.0 copy-done.1
  497.9 1.0 copy.20
  498.8 0.0 copy-done
  498.8 1.0 copy.21
  (1 shorter events, 0.0 us)
Async XLA Ops:
  489.8 8.1 %copy-start.1 = (bf16[4096,128]{1,0:T(8,128)(2,1)S(1)}, bf16[4096,128]{1,0:T(8,128)(2,1)}, u32[]{:S(2)}) copy-start(bf16[4096,128]{1,0:T(8,128)(2,1)} %get-tuple-element.15.k0_hbm) | copy-start | bytes 3145732
  489.8 9.0 %copy-start = (bf16[4096,128]{1,0:T(8,128)(2,1)S(1)}, bf16[4096,128]{1,0:T(8,128)(2,1)}, u32[]{:S(2)}) copy-start(bf16[4096,128]{1,0:T(8,128)(2,1)} %get-tuple-element.16.v0_hbm) | copy-start | bytes 3145732

commit v4 on v3

--- a/solution.py
+++ b/solution.py
@@ -13,9 +13,12 @@
 SCALE_LOG2E = HEAD_DIM ** -0.5 * 1.4426950408889634
 NEG = -1e30
 BQ = 512
-BK = 1024
-WOP = 128
-WOY = 2
+BK = 2048
+Y1 = (0, 272)
+Y2 = ((272, 128), (400, 112))
+YX = (480, 32)
+XP = ((0, 144), (144, 128), (272, 128), (400, 80))
+LATE_ROWS = 128
 MESH = pl.DeviceIdType.MESH
 F32 = jnp.float32
 BF16 = jnp.bfloat16
@@ -29,10 +32,10 @@
 
 def _tables(pos):
     half = HEAD_DIM // 2
-    inv = ROPE_BASE ** (-2.0 * jnp.arange(half, dtype=F32) / HEAD_DIM)
+    lane = jnp.arange(HEAD_DIM)
+    inv = ROPE_BASE ** (-2.0 * (lane % half).astype(F32) / HEAD_DIM)
     ang = pos.astype(F32)[:, None] * inv
-    c, s = jnp.cos(ang), jnp.sin(ang)
-    return jnp.concatenate([c, c], axis=1), jnp.concatenate([-s, s], axis=1)
+    return jnp.cos(ang), jnp.where(lane < half, -1.0, 1.0) * jnp.sin(ang)
 
 
 def _barrier(peers):
@@ -46,9 +49,9 @@
     return [(s + 2) % 4, 3 - s, s + 1 - 2 * (s % 2), s]
 
 
-def _wo_y(tp, s, rep, wo_hbm, wo_dst, ssem, rsem, k, nr):
-    r0 = pl.multiple_of(s * (wo_hbm.shape[0] // 4) + k * nr, 128)
-    return pltpu.make_async_remote_copy(src_ref=wo_hbm.at[pl.ds(r0, nr), :], dst_ref=wo_dst.at[pl.ds(r0, nr), :],
+def _wo_y(rep, tp, s, wo_hbm, wo_dst, quarter, piece, ssem, rsem):
+    r0 = pl.multiple_of(quarter * (wo_hbm.shape[0] // 4) + piece[0], 16)
+    return pltpu.make_async_remote_copy(src_ref=wo_hbm.at[pl.ds(r0, piece[1]), :], dst_ref=wo_dst.at[pl.ds(r0, piece[1]), :],
                                         send_sem=ssem, recv_sem=rsem, device_id=(rep, 1 - tp, s), device_id_type=MESH)
 
 
@@ -86,62 +89,70 @@
     qcopy(0).start()
     qcopy(1).start()
     _barrier([(rep, tp, far), (rep, tp, diag), (rep, tp, mate), (rep, 1 - tp, s)])
-    wo_sends = [_wo_y(tp, s, rep, wo_hbm, wo_dst, wosem.at[k], worsem.at[k], k, WOP) for k in range(WOY)]
-    for c in wo_sends:
-        c.start()
-    for b in range(nb):
-        xc[b].wait()
-
-        @pl.loop(0, rows // 64)
-        def _(i, b=b):
-            xs = xbuf[b, pl.ds(pl.multiple_of(i * 64, 64), 64), :].astype(F32)
-            r = lax.rsqrt(jnp.mean(xs * xs, axis=-1, keepdims=True) + EPS)
-            u[pl.ds(pl.multiple_of(b * rows + i * 64, 64), 64), :] = (xs * r * g_ref[...]).astype(BF16)
-
+    wo_send = _wo_y(rep, tp, s, wo_hbm, wo_dst, s, Y1, wosem.at[0], worsem.at[0])
+    wo_send.start()
     def rope(t, r0):
         c = cos_ref[pl.ds(r0, t.shape[0]), :]
         sn = sin_ref[pl.ds(r0, t.shape[0]), :]
         return t * c + pltpu.roll(t, 64, 1) * sn
 
-    dst = pl.ds(pl.multiple_of(s * m, 128), m)
-
-    def remote(t, sl, j):
+    hm = m // 2
+
+    def kvpair(t, sl, h):
         pair = ((ko, k0_hbm), (vo, v0_hbm)) if sl == 0 else ((ko, k1_hbm), (vo, v1_hbm))
-        return [pltpu.make_async_remote_copy(src_ref=a.at[t], dst_ref=b.at[dst, :], send_sem=ssem.at[sl, t, i], recv_sem=rsem.at[sl, t, i],
-                                             device_id=(rep, tp, j), device_id_type=MESH) for i, (a, b) in enumerate(pair)]
-
-    def local(t, sl):
-        pair = ((ko, k0_hbm), (vo, v0_hbm)) if sl == 0 else ((ko, k1_hbm), (vo, v1_hbm))
-        return [pltpu.make_async_copy(a.at[t], b.at[dst, :], lsem.at[sl, i]) for i, (a, b) in enumerate(pair)]
+        dst = pl.ds(pl.multiple_of(s * m + h * hm, 128), hm)
+        return [(a.at[t, pl.ds(h * hm, hm), :], b.at[dst, :]) for a, b in pair]
+
+    def remote(t, sl, j, h):
+        return [pltpu.make_async_remote_copy(src_ref=a, dst_ref=b, send_sem=ssem.at[sl, t, h, i], recv_sem=rsem.at[sl, t, h, i],
+                                             device_id=(rep, tp, j), device_id_type=MESH) for i, (a, b) in enumerate(kvpair(t, sl, h))]
+
+    def local(t, sl, h):
+        return [pltpu.make_async_copy(a, b, lsem.at[sl, h, i]) for i, (a, b) in enumerate(kvpair(t, sl, h))]
 
     sends = [[(0, far, False)], [(0, diag, False), (1, mate, False)], [(0, mate, False), (1, diag, True)], [(1, far, True)]]
+    def norm(b):
+        xc[b].wait()
+
+        @pl.loop(0, rows // 64)
+        def _(i):
+            xs = xbuf[b, pl.ds(pl.multiple_of(i * 64, 64), 64), :].astype(F32)
+            r = lax.rsqrt(jnp.mean(xs * xs, axis=-1, keepdims=True) + EPS)
+            u[pl.ds(pl.multiple_of(b * rows + i * 64, 64), 64), :] = (xs * r * g_ref[...]).astype(BF16)
+
     for t in range(4):
         sl = t % 2
-        for c in kvcopies(t):
-            c.wait()
-
-        @pl.loop(0, m // 256)
-        def _(i, t=t, sl=sl):
-            r0 = pl.multiple_of(i * 256, 256)
-            kv = jnp.dot(u[pl.ds(r0, 256), :], wkv[sl], preferred_element_type=F32)
-            ko[t, pl.ds(r0, 256), :] = rope(kv[:, :128], r0).astype(BF16)
-            vo[t, pl.ds(r0, 256), :] = kv[:, 128:].astype(BF16)
-        for slot, j, x0_only in sends[t]:
-            def go(t=t, slot=slot, j=j):
-                for c in remote(t, slot, j):
+        if t > 0:
+            for c in kvcopies(t):
+                c.wait()
+        for h in range(2):
+            if t == 0:
+                norm(2 * h)
+                norm(2 * h + 1)
+                if h == 0:
+                    for c in kvcopies(0):
+                        c.wait()
+
+            @pl.loop(h * 2, h * 2 + 2)
+            def _(i, t=t, sl=sl):
+                r0 = pl.multiple_of(i * 256, 256)
+                kv = jnp.dot(u[pl.ds(r0, 256), :], wkv[sl], preferred_element_type=F32)
+                ko[t, pl.ds(r0, 256), :] = rope(kv[:, :128], r0).astype(BF16)
+                vo[t, pl.ds(r0, 256), :] = kv[:, 128:].astype(BF16)
+            for slot, j, x0_only in sends[t]:
+                def go(t=t, slot=slot, j=j, h=h):
+                    for c in remote(t, slot, j, h):
+                        c.start()
+                if x0_only:
+                    pl.when(on_x0)(go)
+                else:
+                    go()
+            if t == 0 or t == 3:
+                for c in local(t, 1 if t == 0 else 0, h):
                     c.start()
-            if x0_only:
-                pl.when(on_x0)(go)
-            else:
-                go()
-        if t == 0 or t == 3:
-            for c in local(t, 1 if t == 0 else 0):
-                c.start()
         if t < 2:
             for c in kvcopies(t + 2):
                 c.start()
-
-    hm = m // 2
 
     def qmove(t, h):
         src = qo.at[t, pl.ds(h * hm, hm), :]
@@ -168,26 +179,26 @@
     for t in range(4):
         for h in range(2):
             qmove(t, h).wait()
-    for c in local(0, 1) + local(3, 0):
-        c.wait()
-    for t in range(4):
-        for slot, j, x0_only in sends[t]:
-            cs = remote(t, slot, j)
-            if x0_only:
-                @pl.when(on_x0)
-                def _(cs=cs):
+    for h in range(2):
+        for c in local(0, 1, h) + local(3, 0, h):
+            c.wait()
+        for t in range(4):
+            for slot, j, x0_only in sends[t]:
+                cs = remote(t, slot, j, h)
+                if x0_only:
+                    @pl.when(on_x0)
+                    def _(cs=cs):
+                        for c in cs:
+                            c.wait_send()
+
+                    @pl.when(jnp.logical_not(on_x0))
+                    def _(cs=cs):
+                        for c in cs:
+                            c.wait_recv()
+                else:
                     for c in cs:
-                        c.wait_send()
-
-                @pl.when(jnp.logical_not(on_x0))
-                def _(cs=cs):
-                    for c in cs:
-                        c.wait_recv()
-            else:
-                for c in cs:
-                    c.wait()
-    for c in wo_sends:
-        c.wait()
+                        c.wait()
+    wo_send.wait()
 
 
 def _qkv(x, g1, cos, sin, wq, wk, wv, wo, n):
@@ -211,13 +222,13 @@
             pltpu.VMEM((4, m, 128), BF16),
             pltpu.SemaphoreType.DMA((4,)),
             pltpu.SemaphoreType.DMA((2, 3)),
-            pltpu.SemaphoreType.DMA((2, 4, 2)),
-            pltpu.SemaphoreType.DMA((2, 4, 2)),
-            pltpu.SemaphoreType.DMA((2, 2)),
+            pltpu.SemaphoreType.DMA((2, 4, 2, 2)),
+            pltpu.SemaphoreType.DMA((2, 4, 2, 2)),
+            pltpu.SemaphoreType.DMA((2, 2, 2)),
             pltpu.SemaphoreType.DMA((4, 2)),
             pltpu.SemaphoreType.DMA((2, 2)),
-            pltpu.SemaphoreType.DMA((4,)),
-            pltpu.SemaphoreType.DMA((4,)),
+            pltpu.SemaphoreType.DMA((1,)),
+            pltpu.SemaphoreType.DMA((1,)),
         ],
         compiler_params=pltpu.CompilerParams(collective_id=1, has_side_effects=True, vmem_limit_bytes=56 * 2**20),
         cost_estimate=pl.CostEstimate(flops=2 * m * d * (4 * qw + 1024), bytes_accessed=80 * 2**20, transcendentals=0),
@@ -230,8 +241,8 @@
     return t % 2, i % 2, (tp + i // 2) % 2
 
 
-def _attn_body(q_ref, k0_hbm, v0_hbm, k1_hbm, v1_hbm, wo_hbm, woi_hbm, own_hbm, oth_hbm, wo_dst, late_hbm,
-               kb, vb, vt, acc, ms, ls, ob, kvsem, ssem, rsem0, rsem1, lsem, lasem, wsem, wrsem):
+def _attn_body(q_ref, k0_hbm, v0_hbm, k1_hbm, v1_hbm, wo_hbm, woi_hbm, own_hbm, oth_hbm, wo_dst, late_hbm, late2_hbm,
+               kb, vb, vt, eye, acc, ms, ls, ob, kvsem, ssem, rsem0, rsem1, lsem, lasem, l2sem, wsem, wrsem):
     rep, tp, s = lax.axis_index("rep"), lax.axis_index("tp"), lax.axis_index("sp")
     step = pl.program_id(0)
     order = _sp_order(s)
@@ -244,14 +255,23 @@
     r = 2 * cc + half
     nk = kb.shape[1]
 
-    wo_y = [_wo_y(tp, s, rep, wo_hbm, wo_dst, wsem.at[0, k], wrsem.at[0, k], k, WOP) for k in range(WOY, 4)]
-
-    def wo_piece(kind, k):
-        quarter = far if kind == 3 else s
-        r0 = pl.multiple_of(quarter * qr + k * WOP, 128)
-        return pltpu.make_async_remote_copy(src_ref=wo_dst.at[pl.ds(r0, WOP), :], dst_ref=wo_dst.at[pl.ds(r0, WOP), :],
+    wo_y = [_wo_y(rep, tp, s, wo_hbm, wo_dst, s, p, wsem.at[0, k], wrsem.at[0, k]) for k, p in enumerate(Y2)]
+    wo_y.append(_wo_y(rep, tp, s, wo_hbm, wo_dst, far, YX, wsem.at[0, 2], wrsem.at[0, 2]))
+
+    def wo_move(quarter, piece, peer, kind, k):
+        r0 = pl.multiple_of(quarter * qr + piece[0], 16)
+        return pltpu.make_async_remote_copy(src_ref=wo_dst.at[pl.ds(r0, piece[1]), :], dst_ref=wo_dst.at[pl.ds(r0, piece[1]), :],
                                             send_sem=wsem.at[kind, k], recv_sem=wrsem.at[kind, k],
-                                            device_id=(rep, tp, far if kind == 1 else mate), device_id_type=MESH)
+                                            device_id=(rep, tp, peer), device_id_type=MESH)
+
+    def wo_x(k):
+        return wo_move(s, XP[k], far, 1, k)
+
+    def wo_near(k):
+        return wo_move(s, (Y1, *Y2)[k], mate, 2, k)
+
+    def wo_near_far(k):
+        return wo_move(far, (*XP, YX)[k], mate, 3, k)
 
     def kv_copies(g):
         return [pltpu.make_async_copy((k0_hbm, k1_hbm)[g], kb.at[g], kvsem.at[g, 0]),
@@ -265,9 +285,10 @@
         _barrier([(rep, tp, far), (rep, tp, mate), (rep, 1 - tp, s), (rep, 1 - tp, mate)])
         for c in wo_y:
             c.start()
-        for k in range(WOY):
-            wo_piece(1, k).start()
-            wo_piece(2, k).start()
+        wo_x(0).start()
+        wo_x(1).start()
+        wo_near(0).start()
+        eye[...] = (lax.broadcasted_iota(jnp.int32, eye.shape, 0) == lax.broadcasted_iota(jnp.int32, eye.shape, 1)).astype(F32).astype(BF16)
         for g in range(2):
             for c in kv_copies(g):
                 c.wait()
@@ -275,7 +296,8 @@
             @pl.loop(0, nk // 512)
             def _(j, g=g):
                 r0 = pl.multiple_of(j * 512, 512)
-                vt[g, :, pl.ds(r0, 512)] = vb[g, pl.ds(r0, 512), :].T
+                vt[g, :, pl.ds(r0, 512)] = lax.dot_general(
+                    eye[:128, :128], vb[g, pl.ds(r0, 512), :], (((1,), (1,)), ((), ())), preferred_element_type=F32).astype(BF16)
 
     ms[...] = jnp.full_like(ms, NEG)
     ls[...] = jnp.zeros_like(ls)
@@ -299,7 +321,7 @@
                 sc = jnp.where(qq >= kk, sc, NEG)
             m0 = ms[h:h + 1, :]
             m1 = jnp.maximum(m0, jnp.max(sc, axis=0, keepdims=True))
-            p = jnp.exp2(sc * SCALE_LOG2E - m1 * SCALE_LOG2E)
+            p = jnp.exp2((sc - m1) * SCALE_LOG2E)
             a = jnp.exp2((m0 - m1) * SCALE_LOG2E)
             ms[h:h + 1, :] = m1
             ls[h:h + 1, :] = ls[h:h + 1, :] * a + jnp.sum(p, axis=0, keepdims=True)
@@ -310,14 +332,19 @@
     def _(j):
         blk(j * BK, BK, False)
 
-    @pl.when(start % BK != 0)
+    @pl.when(start // 1024 % 2 == 1)
+    def _():
+        blk(start // BK * BK, 1024, False)
+
+    @pl.when(start // BQ % 2 == 1)
     def _():
         blk(start - BQ, BQ, False)
 
     blk(start, BQ, True)
     for h in range(nh):
         o = acc[h] * (1.0 / ls[h:h + 1, :])
-        ob[step, :, h * 128:(h + 1) * 128] = o.T.astype(BF16)
+        ob[step, :, h * 128:(h + 1) * 128] = lax.dot_general(
+            eye[...], o.astype(BF16), (((1,), (1,)), ((), ())), preferred_element_type=F32).astype(BF16)
 
     w = q_ref.shape[2]
 
@@ -339,19 +366,32 @@
         slot = (half + tp + 1) % 2
         return pltpu.make_async_copy(ob.at[t], dst(own_hbm, slot, s, g), lsem.at[g, half])
 
-    def to_oth(t):
-        g, cc, _ = _place(t, tp)
+    def first_rows(g):
+        return BQ if g == 0 else BQ - LATE_ROWS
+
+    def to_oth(t, g):
+        cc, nr = _place(t, tp)[1], first_rows(g)
         return pltpu.make_async_remote_copy(
-            src_ref=ob.at[t], dst_ref=oth_hbm.at[:, cols(s, g)], send_sem=ssem.at[1, t], recv_sem=rsem1.at[s % 2, g],
+            src_ref=ob.at[t, pl.ds(0, nr), :], dst_ref=oth_hbm.at[pl.ds(0, nr), cols(s, g)],
+            send_sem=ssem.at[1, t], recv_sem=rsem1.at[s % 2, g],
             device_id=(rep, 1 - tp, s // 2 * 2 + cc), device_id_type=MESH)
+
+    def to_late2(t):
+        cc = _place(t, tp)[1]
+        return pltpu.make_async_copy(ob.at[t, pl.ds(BQ - LATE_ROWS, LATE_ROWS), :], late2_hbm.at[cc], l2sem.at[cc])
 
     def to_late(t):
         g, cc, _ = _place(t, tp)
         return pltpu.make_async_copy(ob.at[t], late_hbm.at[g, cc], lasem.at[g, cc])
 
-    @pl.when(step < 4)
-    def _():
-        to_oth(step).start()
+    @pl.when((step < 4) & (grp == 0))
+    def _():
+        to_oth(step, 0).start()
+
+    @pl.when((step < 4) & (grp == 1))
+    def _():
+        to_oth(step, 1).start()
+        to_late2(step).start()
 
     @pl.when(step >= 4)
     def _():
@@ -368,28 +408,38 @@
     def _():
         to_own(step).start()
 
-    for k in range(WOY, 4):
-        @pl.when(step == 2 * (k - WOY) + 2)
+    @pl.when(step == 2)
+    def _():
+        wo_y[0].wait_recv()
+        wo_x(2).start()
+        wo_near(1).start()
+        wo_x(0).wait_recv()
+        wo_near_far(0).start()
+
+    @pl.when(step == 4)
+    def _():
+        wo_y[1].wait_recv()
+        wo_x(3).start()
+        wo_near(2).start()
+        wo_y[2].wait_recv()
+        wo_near_far(4).start()
+
+    for k in (1, 2):
+        @pl.when(step == 4 + k)
         def _(k=k):
-            wo_y[k - WOY].wait_recv()
-            wo_piece(1, k).start()
-            wo_piece(2, k).start()
-
-    for k in range(3):
-        @pl.when(step == 2 * k + 2)
-        def _(k=k):
-            wo_piece(1, k).wait_recv()
-            wo_piece(3, k).start()
+            wo_x(k).wait_recv()
+            wo_near_far(k).start()
 
     @pl.when(step == pl.num_programs(0) - 1)
     def _():
-        wo_piece(1, 3).wait_recv()
-        wo_piece(3, 3).start()
-
-        @pl.loop(0, 4)
-        def _(t):
-            to_oth(t).wait_send()
+        wo_x(3).wait_recv()
+        wo_near_far(3).start()
+
+        for t in range(4):
+            to_oth(t, t % 2).wait_send()
             to_late(t + 4).wait()
+        to_late2(1).wait()
+        to_late2(3).wait()
 
         @pl.loop(0, 8)
         def _(t):
@@ -409,14 +459,17 @@
             for core in range(2):
                 src_s = s // 2 * 2 + core
                 pltpu.make_async_remote_copy(
-                    src_ref=ob.at[0], dst_ref=oth_hbm.at[:, cols(src_s, g)], send_sem=ssem.at[1, 0], recv_sem=rsem1.at[core, g],
+                    src_ref=ob.at[0, pl.ds(0, first_rows(g)), :], dst_ref=oth_hbm.at[pl.ds(0, first_rows(g)), cols(src_s, g)],
+                    send_sem=ssem.at[1, 0], recv_sem=rsem1.at[core, g],
                     device_id=(rep, 1 - tp, src_s), device_id_type=MESH).wait_recv()
         for c in wo_y:
             c.wait_send()
         for k in range(4):
-            wo_piece(1, k).wait_send()
-            wo_piece(2, k).wait()
-            wo_piece(3, k).wait()
+            wo_x(k).wait_send()
+        for k in range(3):
+            wo_near(k).wait()
+        for k in range(5):
+            wo_near_far(k).wait()
 
 
 def _attention(q, k0, v0, k1, v1, wo, wo_oth):
@@ -430,14 +483,15 @@
         _attn_body,
         grid=(steps,),
         in_specs=[pl.BlockSpec((1, BQ, w), lambda t: (t % 2, t // 2, 0))] + [any_] * 6,
-        out_specs=[any_] * 4,
+        out_specs=[any_] * 5,
         out_shape=[shape, jax.ShapeDtypeStruct((BQ, 4 * w), BF16), jax.ShapeDtypeStruct(wo.shape, BF16),
-                   jax.ShapeDtypeStruct((2, 2, BQ, w), BF16)],
+                   jax.ShapeDtypeStruct((2, 2, BQ, w), BF16), jax.ShapeDtypeStruct((2, LATE_ROWS, w), BF16)],
         input_output_aliases={6: 2},
         scratch_shapes=[
             pltpu.VMEM((2, n, 128), BF16),
             pltpu.VMEM((2, n, 128), BF16),
             pltpu.VMEM((2, 128, n), BF16),
+            pltpu.VMEM((BQ, BQ), BF16),
             pltpu.VMEM((nh, 128, BQ), F32),
             pltpu.VMEM((8, BQ), F32),
             pltpu.VMEM((8, BQ), F32),
@@ -448,8 +502,9 @@
             pltpu.SemaphoreType.DMA((2, 2)),
             pltpu.SemaphoreType.DMA((2, 2)),
             pltpu.SemaphoreType.DMA((2, 2)),
-            pltpu.SemaphoreType.DMA((4, 4)),
-            pltpu.SemaphoreType.DMA((4, 4)),
+            pltpu.SemaphoreType.DMA((2,)),
+            pltpu.SemaphoreType.DMA((4, 5)),
+            pltpu.SemaphoreType.DMA((4, 5)),
         ],
         compiler_params=pltpu.CompilerParams(collective_id=2, has_side_effects=True, vmem_limit_bytes=56 * 2**20),
         cost_estimate=pl.CostEstimate(flops=2 * n * n * w * 2, bytes_accessed=16 * 2**20, transcendentals=0),
@@ -463,8 +518,8 @@
 MB = 256
 
 
-def _mlp_body(chunks, own_hbm, oth_hbm, x_hbm, wo_hbm, wo_oth_hbm, g_ref, w1_hbm, w3_hbm, w2_hbm, late_hbm, y_hbm, olate_hbm,
-              wb, abuf, xbuf, hid, pbuf, rbuf, ybuf, wsem, asem, ssem, rsem, ysem, yrsem, ylsem, lasem, larsem):
+def _mlp_body(chunks, own_hbm, oth_hbm, x_hbm, wo_hbm, wo_oth_hbm, g_ref, w1_hbm, w3_hbm, w2_hbm, late_hbm, late2_hbm, y_hbm, olate_hbm, olate2_hbm,
+              wb, abuf, xbuf, hid, pbuf, rbuf, ybuf, wsem, asem, ssem, rsem, ysem, yrsem, ylsem, lasem, larsem, l2sem, l2rsem):
     rep, tp, s = lax.axis_index("rep"), lax.axis_index("tp"), lax.axis_index("sp")
     hr = wo_hbm.shape[0]
     hm = x_hbm.shape[0] // 2
@@ -510,9 +565,22 @@
         slot, r0, nr = chunks[c]
         base = hm * ((tp + slot + 1) % 2) + r0
         rs = pl.ds(0, nr)
-        return (pltpu.make_async_copy(x_hbm.at[pl.ds(pl.multiple_of(base, 128), nr), :], xbuf.at[rs, :], asem.at[0]),
-                [pltpu.make_async_copy(own_hbm.at[slot, pl.ds(r0, nr), :], abuf.at[rs, pl.ds(0, hr)], asem.at[1]),
-                 pltpu.make_async_copy((oth_hbm if slot == 0 else olate_hbm).at[pl.ds(r0, nr), :], abuf.at[rs, pl.ds(hr, hr)], asem.at[2])])
+        xcopy = pltpu.make_async_copy(x_hbm.at[pl.ds(pl.multiple_of(base, 128), nr), :], xbuf.at[rs, :], asem.at[0])
+        cs = [pltpu.make_async_copy(own_hbm.at[slot, pl.ds(r0, nr), :], abuf.at[rs, pl.ds(0, hr)], asem.at[1])]
+        late_at = hm - LATE_ROWS
+        if slot == 1:
+            cs.append(pltpu.make_async_copy(olate_hbm.at[pl.ds(r0, nr), :], abuf.at[rs, pl.ds(hr, hr)], asem.at[2]))
+        elif r0 + nr <= late_at:
+            cs.append(pltpu.make_async_copy(oth_hbm.at[pl.ds(r0, nr), :], abuf.at[rs, pl.ds(hr, hr)], asem.at[2]))
+        else:
+            n0 = late_at - r0
+            c0 = pl.multiple_of(s // 2 * (hr // 2), 128)
+            c1 = pl.multiple_of((1 - s // 2) * (hr // 2), 128)
+            ls = pl.ds(n0, LATE_ROWS)
+            cs.append(pltpu.make_async_copy(oth_hbm.at[pl.ds(r0, n0), :], abuf.at[pl.ds(0, n0), pl.ds(hr, hr)], asem.at[2]))
+            cs.append(pltpu.make_async_copy(oth_hbm.at[pl.ds(late_at, LATE_ROWS), pl.ds(c0, hr // 2)], abuf.at[ls, pl.ds(hr + c0, hr // 2)], asem.at[3]))
+            cs.append(pltpu.make_async_copy(olate2_hbm, abuf.at[ls, pl.ds(hr + c1, hr // 2)], asem.at[4]))
+        return xcopy, cs
 
     for g in range(NBUF - 1):
         issue(g)
@@ -530,6 +598,14 @@
             send_sem=lasem.at[g, cc], recv_sem=larsem.at[g, src_s % 2],
             device_id=(rep, 1 - tp, s // 2 * 2 + cc), device_id_type=MESH)
 
+    def late2(cc, src_s):
+        return pltpu.make_async_remote_copy(
+            src_ref=late2_hbm.at[cc], dst_ref=olate2_hbm.at[:, pl.ds(pl.multiple_of(src_s % 2 * w, 128), w)],
+            send_sem=l2sem.at[cc], recv_sem=l2rsem.at[src_s % 2],
+            device_id=(rep, 1 - tp, s // 2 * 2 + cc), device_id_type=MESH)
+
+    for cc in range(2):
+        late2(cc, s).start()
     for g in range(2):
         for cc in range(2):
             late(g, cc, s).start()
@@ -595,6 +671,9 @@
                 a = ab[:, :256]
                 hid[rs, col(j, 256)] = (a / (1.0 + jnp.exp(-a)) * ab[:, 256:]).astype(BF16)
 
+        if ci + 3 == len(chunks):
+            for core in range(2):
+                late2(core, s // 2 * 2 + core).wait_recv()
         if ci + 2 == len(chunks):
             for g in range(2):
                 for core in range(2):
@@ -631,8 +710,9 @@
                 ysend(j).start()
                 yown(j).start()
 
-    for g in range(2):
-        for cc in range(2):
+    for cc in range(2):
+        late2(cc, s).wait_send()
+        for g in range(2):
             late(g, cc, s).wait_send()
 
     @pl.loop(0, NW2 // 2)
@@ -644,7 +724,7 @@
         yrecv(j).wait_recv()
 
 
-def _mlp(own, oth, late, x, wo, wo_oth, g2, w1, w3, w2):
+def _mlp(own, oth, late, late2, x, wo, wo_oth, g2, w1, w3, w2):
     m, d = x.shape
     hm = m // 2
     chunks = ((0, 0, 256), (0, 256, 256), (1, 0, 512))
@@ -653,9 +733,10 @@
     nt = NW2 // 2
     return pl.pallas_call(
         functools.partial(_mlp_body, chunks),
-        in_specs=[any_] * 5 + [vm] + [any_] * 4,
-        out_specs=[any_, any_],
-        out_shape=[jax.ShapeDtypeStruct((m, d), BF16), jax.ShapeDtypeStruct((hm, wo.shape[0]), BF16)],
+        in_specs=[any_] * 5 + [vm] + [any_] * 5,
+        out_specs=[any_] * 3,
+        out_shape=[jax.ShapeDtypeStruct((m, d), BF16), jax.ShapeDtypeStruct((hm, wo.shape[0]), BF16),
+                   jax.ShapeDtypeStruct((LATE_ROWS, wo.shape[0] // 2), BF16)],
         scratch_shapes=[
             pltpu.VMEM((NBUF, d, 512), BF16),
             pltpu.VMEM((hm, d), BF16),
@@ -665,7 +746,7 @@
             pltpu.VMEM((nt, hm, 512), F32),
             pltpu.VMEM((nt, hm, 512), BF16),
             pltpu.SemaphoreType.DMA((NBUF, 2)),
-            pltpu.SemaphoreType.DMA((3,)),
+            pltpu.SemaphoreType.DMA((5,)),
             pltpu.SemaphoreType.DMA((2, nt)),
             pltpu.SemaphoreType.DMA((2, nt)),
             pltpu.SemaphoreType.DMA((nt,)),
@@ -673,11 +754,43 @@
             pltpu.SemaphoreType.DMA((nt,)),
             pltpu.SemaphoreType.DMA((2, 2)),
             pltpu.SemaphoreType.DMA((2, 2)),
+            pltpu.SemaphoreType.DMA((2,)),
+            pltpu.SemaphoreType.DMA((2,)),
         ],
         compiler_params=pltpu.CompilerParams(collective_id=3, has_side_effects=True, vmem_limit_bytes=67043328),
         cost_estimate=pl.CostEstimate(flops=2 * m * d * (d + 3 * w1.shape[1]), bytes_accessed=640 * 2**20, transcendentals=0),
         name="mlp_sum",
-    )(own, oth, x, wo, wo_oth, g2.reshape(1, -1), w1, w3, w2, late)[0]
+    )(own, oth, x, wo, wo_oth, g2.reshape(1, -1), w1, w3, w2, late, late2)[0]
+
+
+def _copy_body(y_ref, k_ref, v_ref, yo_ref, ko_ref, vo_ref, buf, kbuf, sem):
+    n, nr = buf.shape[:2]
+    moves = [(y_ref.at[pl.ds(i * nr, nr), :], yo_ref.at[pl.ds(i * nr, nr), :], buf.at[i]) for i in range(n)]
+    moves += [(k_ref, ko_ref, kbuf.at[0]), (v_ref, vo_ref, kbuf.at[1])]
+    get = [pltpu.make_async_copy(a, b, sem.at[0, i]) for i, (a, _, b) in enumerate(moves)]
+    put = [pltpu.make_async_copy(b, c, sem.at[1, i]) for i, (_, c, b) in enumerate(moves)]
+    for c in get:
+        c.start()
+    for g, p in zip(get, put):
+        g.wait()
+        p.start()
+    for p in put:
+        p.wait()
+
+
+def _copy(*arrays):
+    y, k, _ = arrays
+    m, d = y.shape
+    any_ = pl.BlockSpec(memory_space=pl.ANY)
+    return pl.pallas_call(
+        _copy_body,
+        in_specs=[any_] * 3,
+        out_specs=[any_] * 3,
+        out_shape=[jax.ShapeDtypeStruct(a.shape, a.dtype) for a in arrays],
+        scratch_shapes=[pltpu.VMEM((8, m // 8, d), BF16), pltpu.VMEM((2, *k.shape), BF16), pltpu.SemaphoreType.DMA((2, 10))],
+        compiler_params=pltpu.CompilerParams(vmem_limit_bytes=67043328),
+        name="result_copy",
+    )(*arrays)
 
 
 def solution(mesh):
@@ -691,8 +804,9 @@
         n = m * mesh.shape["sp"]
         cos, sin = _tables(pos)
         q, k, v, k1, v1, wo_oth = _qkv(x, g1, cos, sin, wq, wk, wv, wo, n)
-        own, oth, wo_oth, late = _attention(q, k, v, k1, v1, wo, wo_oth)
-        y = _mlp(own, oth, late, x, wo, wo_oth, g2, w1, w3, w2)
+        own, oth, wo_oth, late, late2 = _attention(q, k, v, k1, v1, wo, wo_oth)
+        y = _mlp(own, oth, late, late2, x, wo, wo_oth, g2, w1, w3, w2)
+        y, k, v = _copy(y, k, v)
         return y, k.reshape(n, 1, 128), v.reshape(n, 1, 128)
 
     return jax.shard_map(

time: 500 us -> 489 us (0.978)
  local copies, waits for them, and re-layouts: 9.98 us -> 0 us
    unnamed x7 -> x0, local copies, waits for them, and re-layouts: 9.98 us -> none
    pallas_call x0 -> x1, Pallas kernels: none -> 8.19 us  [_copy(): pl.pallas_call(_copy_body, in_specs=[any_] * 3, out_specs=[any_] * 3, out...]
    pallas_call x1, Pallas kernels: 99.8 us -> 92.3 us  [_attention(): pl.pallas_call(_attn_body, grid=(steps,), in_specs=[pl.BlockSpec((1, BQ,...]
where the time goes in v4:
time: 489 us; the launch traced here: 488 us
  Pallas kernels  483 us (99%)
    pallas_call x1, Pallas kernels, _mlp(): pl.pallas_call(functools.partial(_mlp_body, chunks), in_specs=[any_] * 5...  327 us
    pallas_call x1, Pallas kernels, _attention(): pl.pallas_call(_attn_body, grid=(steps,), in_specs=[pl.BlockSpec((1, BQ,...  92.3 us
    pallas_call x1, Pallas kernels, _qkv(): pl.pallas_call(_qkv_body, in_specs=[any_, vm, vm, vm, any_, any_, any_, a...  55.7 us

profile of v4, /device:TPU:0, one launch (start us, length us, event | category | flops | bytes accessed | tf_op | source)
XLA Modules:
  0.0 488.0 jit_solution(17207387790214180861)
XLA Ops:
  0.6 0.7 convert_element_type.10
  1.3 3.0 fusion
  4.4 55.7 %qkv_exchange.1 = (bf16[2,2048,512]{2,1,0:T(8,128)(2,1)}, bf16[4096,128]{1,0:T(8,128)(2,1)}, bf16[4096,128]{1,0:T(8,128)(2,1)}, bf16[4096,128]{1,0:T(8,128)(2,1)...) custom-call(bf16[1024,4096]{1,0:T(8,128)(2,1)} %x_hbm.3, f32[1,4096]{1,0:T(1,128)} %bitcast.6, ...), custom_call_target="tpu_custom_call" | custom-call | flops 25769803776 | bytes 83886080 | tf_op jit(solution)/shard_map/qkv_exchange/pallas_call | solution.py:210
  60.0 92.3 %attention_exchange.1 = (bf16[2,512,2048]{2,1,0:T(8,128)(2,1)}, bf16[512,2048]{1,0:T(8,128)(2,1)}, bf16[2048,4096]{1,0:T(8,128)(2,1)}, bf16[2,2,512,512]{3,2,1,0:T(8,128)(2,1)}, bf16[2,128,512]{2,1,0:T(8,128)(2,1)}) custom-call(bf16[2,2048,512]{2,1,0:T(8,128)(2,1)} %get-tuple-element.18.q_ref, ...), custom_call_target="tpu_custom_call", output_to_operand_aliasing={{2}: (6, {})} | custom-call | flops 34359738368 | bytes 16777216 | tf_op jit(solution)/shard_map/attention_exchange/pallas_call | solution.py:482
  152.3 327.3 %mlp_sum.1 = (bf16[1024,4096]{1,0:T(8,128)(2,1)}, bf16[512,2048]{1,0:T(8,128)(2,1)}, bf16[128,1024]{1,0:T(8,128)(2,1)}) custom-call(bf16[2,512,2048]{2,1,0:T(8,128)(2,1)} %get-tuple-element.24.own_hbm, bf16[512,2048]{1,0:T(8,128)(2,1)} %get-tuple-element.25.oth_hbm, bf16[1024,4096]{1,0:T(8,128)(2,1)} %x_hbm.3, bf16[2048,4096]{1,0:T(8,128)(2,1)} %wo_hbm.5, ...), custom_call_target="tpu_custom_call" | custom-call | flops 214748364800 | bytes 671088640 | tf_op jit(solution)/shard_map/mlp_sum/pallas_call | solution.py:734
  479.6 8.2 %result_copy.1 = (bf16[1024,4096]{1,0:T(8,128)(2,1)}, bf16[4096,128]{1,0:T(8,128)(2,1)}, bf16[4096,128]{1,0:T(8,128)(2,1)}) custom-call(bf16[1024,4096]{1,0:T(8,128)(2,1)} %get-tuple-element.29.y_ref, bf16[4096,128]{1,0:T(8,128)(2,1)} %get-tuple-element.19.k0_hbm.k_ref, bf16[4096,128]{1,0:T(8,128)(2,1)} %get-tuple-element.20.v0_hbm.v_ref), custom_call_target="tpu_custom_call" | custom-call | tf_op jit(solution)/shard_map/result_copy/pallas_call | solution.py:785
  (1 shorter events, 0.0 us)

commit v5 on v4

--- a/solution.py
+++ b/solution.py
@@ -22,6 +22,15 @@
 MESH = pl.DeviceIdType.MESH
 F32 = jnp.float32
 BF16 = jnp.bfloat16
+LANES = 128
+RB = 256
+TILE = 512
+HALF = 64
+SP = 4
+CORES = 2
+MIB = 2**20
+KERNEL_VMEM = 56 * MIB
+MAX_VMEM = 67043328
 
 
 def _rms(x, g):
@@ -46,11 +55,11 @@
 
 
 def _sp_order(s):
-    return [(s + 2) % 4, 3 - s, s + 1 - 2 * (s % 2), s]
+    return [(s + 2) % SP, 3 - s, s + 1 - 2 * (s % CORES), s]
 
 
 def _wo_y(rep, tp, s, wo_hbm, wo_dst, quarter, piece, ssem, rsem):
-    r0 = pl.multiple_of(quarter * (wo_hbm.shape[0] // 4) + piece[0], 16)
+    r0 = pl.multiple_of(quarter * (wo_hbm.shape[0] // SP) + piece[0], 16)
     return pltpu.make_async_remote_copy(src_ref=wo_hbm.at[pl.ds(r0, piece[1]), :], dst_ref=wo_dst.at[pl.ds(r0, piece[1]), :],
                                         send_sem=ssem, recv_sem=rsem, device_id=(rep, 1 - tp, s), device_id_type=MESH)
 
@@ -60,7 +69,7 @@
     rep, tp, s = lax.axis_index("rep"), lax.axis_index("tp"), lax.axis_index("sp")
     order = _sp_order(s)
     far, diag, mate = order[:3]
-    on_x0 = s // 2 == 0
+    on_x0 = s // CORES == 0
     m = u.shape[0]
     nb = xbuf.shape[0]
     rows = m // nb
@@ -69,14 +78,14 @@
     def kvcopies(t):
         j, sl = order[t], t % 2
         return [
-            pltpu.make_async_copy(wk_hbm.at[:, pl.ds(pl.multiple_of(j * 128, 128), 128)], wkv.at[sl, :, pl.ds(0, 128)], wsem.at[sl, 1]),
-            pltpu.make_async_copy(wv_hbm.at[:, pl.ds(pl.multiple_of(j * 128, 128), 128)], wkv.at[sl, :, pl.ds(128, 128)], wsem.at[sl, 2]),
+            pltpu.make_async_copy(wk_hbm.at[:, pl.ds(pl.multiple_of(j * LANES, LANES), LANES)], wkv.at[sl, :, pl.ds(0, LANES)], wsem.at[sl, 1]),
+            pltpu.make_async_copy(wv_hbm.at[:, pl.ds(pl.multiple_of(j * LANES, LANES), LANES)], wkv.at[sl, :, pl.ds(LANES, LANES)], wsem.at[sl, 2]),
         ]
 
-    groups = [mate, (mate + 2) % 4, s, far]
+    groups = [mate, (mate + 2) % SP, s, far]
 
     def qcopy(t):
-        return pltpu.make_async_copy(wq_hbm.at[:, pl.ds(pl.multiple_of(groups[t] * qw, 128), qw)], wq.at[t % 2], wsem.at[t % 2, 0])
+        return pltpu.make_async_copy(wq_hbm.at[:, pl.ds(pl.multiple_of(groups[t] * qw, LANES), qw)], wq.at[t % 2], wsem.at[t % 2, 0])
 
     xc = [pltpu.make_async_copy(x_hbm.at[pl.ds(b * rows, rows), :], xbuf.at[b], xsem.at[b]) for b in range(nb)]
     xc[0].start()
@@ -94,13 +103,13 @@
     def rope(t, r0):
         c = cos_ref[pl.ds(r0, t.shape[0]), :]
         sn = sin_ref[pl.ds(r0, t.shape[0]), :]
-        return t * c + pltpu.roll(t, 64, 1) * sn
+        return t * c + pltpu.roll(t, HALF, 1) * sn
 
     hm = m // 2
 
     def kvpair(t, sl, h):
         pair = ((ko, k0_hbm), (vo, v0_hbm)) if sl == 0 else ((ko, k1_hbm), (vo, v1_hbm))
-        dst = pl.ds(pl.multiple_of(s * m + h * hm, 128), hm)
+        dst = pl.ds(pl.multiple_of(s * m + h * hm, LANES), hm)
         return [(a.at[t, pl.ds(h * hm, hm), :], b.at[dst, :]) for a, b in pair]
 
     def remote(t, sl, j, h):
@@ -114,18 +123,18 @@
     def norm(b):
         xc[b].wait()
 
-        @pl.loop(0, rows // 64)
+        @pl.loop(0, rows // HALF)
         def _(i):
-            xs = xbuf[b, pl.ds(pl.multiple_of(i * 64, 64), 64), :].astype(F32)
+            xs = xbuf[b, pl.ds(pl.multiple_of(i * HALF, HALF), HALF), :].astype(F32)
             r = lax.rsqrt(jnp.mean(xs * xs, axis=-1, keepdims=True) + EPS)
-            u[pl.ds(pl.multiple_of(b * rows + i * 64, 64), 64), :] = (xs * r * g_ref[...]).astype(BF16)
-
-    for t in range(4):
+            u[pl.ds(pl.multiple_of(b * rows + i * HALF, HALF), HALF), :] = (xs * r * g_ref[...]).astype(BF16)
+
+    for t in range(SP):
         sl = t % 2
         if t > 0:
             for c in kvcopies(t):
                 c.wait()
-        for h in range(2):
+        for h in range(CORES):
             if t == 0:
                 norm(2 * h)
                 norm(2 * h + 1)
@@ -135,10 +144,10 @@
 
             @pl.loop(h * 2, h * 2 + 2)
             def _(i, t=t, sl=sl):
-                r0 = pl.multiple_of(i * 256, 256)
-                kv = jnp.dot(u[pl.ds(r0, 256), :], wkv[sl], preferred_element_type=F32)
-                ko[t, pl.ds(r0, 256), :] = rope(kv[:, :128], r0).astype(BF16)
-                vo[t, pl.ds(r0, 256), :] = kv[:, 128:].astype(BF16)
+                r0 = pl.multiple_of(i * RB, RB)
+                kv = jnp.dot(u[pl.ds(r0, RB), :], wkv[sl], preferred_element_type=F32)
+                ko[t, pl.ds(r0, RB), :] = rope(kv[:, :LANES], r0).astype(BF16)
+                vo[t, pl.ds(r0, RB), :] = kv[:, LANES:].astype(BF16)
             for slot, j, x0_only in sends[t]:
                 def go(t=t, slot=slot, j=j, h=h):
                     for c in remote(t, slot, j, h):
@@ -156,33 +165,33 @@
 
     def qmove(t, h):
         src = qo.at[t, pl.ds(h * hm, hm), :]
-        to = q_hbm.at[t % 2, pl.ds(pl.multiple_of(((h + tp) % 2 * 2 + s % 2) * hm, 128), hm), :]
+        to = q_hbm.at[t % 2, pl.ds(pl.multiple_of(((h + tp) % 2 * 2 + s % CORES) * hm, LANES), hm), :]
         if t < 2:
             return pltpu.make_async_remote_copy(src_ref=src, dst_ref=to, send_sem=qsem.at[t, h], recv_sem=qrsem.at[t, h],
                                                 device_id=(rep, tp, mate), device_id_type=MESH)
         return pltpu.make_async_copy(src, to, qsem.at[t, h])
 
-    for t in range(4):
+    for t in range(SP):
         qcopy(t).wait()
 
-        @pl.loop(0, m // 256)
+        @pl.loop(0, m // RB)
         def _(i, t=t):
-            r0 = pl.multiple_of(i * 256, 256)
-            qq = jnp.dot(u[pl.ds(r0, 256), :], wq[t % 2], preferred_element_type=F32)
-            for n in range(qw // 128):
-                qo[t, pl.ds(r0, 256), n * 128:(n + 1) * 128] = rope(qq[:, n * 128:(n + 1) * 128], r0).astype(BF16)
-        for h in range(2):
+            r0 = pl.multiple_of(i * RB, RB)
+            qq = jnp.dot(u[pl.ds(r0, RB), :], wq[t % 2], preferred_element_type=F32)
+            for n in range(qw // LANES):
+                qo[t, pl.ds(r0, RB), n * LANES:(n + 1) * LANES] = rope(qq[:, n * LANES:(n + 1) * LANES], r0).astype(BF16)
+        for h in range(CORES):
             qmove(t, h).start()
         if t < 2:
             qcopy(t + 2).start()
 
-    for t in range(4):
-        for h in range(2):
+    for t in range(SP):
+        for h in range(CORES):
             qmove(t, h).wait()
-    for h in range(2):
+    for h in range(CORES):
         for c in local(0, 1, h) + local(3, 0, h):
             c.wait()
-        for t in range(4):
+        for t in range(SP):
             for slot, j, x0_only in sends[t]:
                 cs = remote(t, slot, j, h)
                 if x0_only:
@@ -203,35 +212,35 @@
 
 def _qkv(x, g1, cos, sin, wq, wk, wv, wo, n):
     m, d = x.shape
-    qw = wq.shape[1] // 4
+    qw = wq.shape[1] // SP
     any_ = pl.BlockSpec(memory_space=pl.ANY)
     vm = pl.BlockSpec(memory_space=pltpu.VMEM)
-    kv = jax.ShapeDtypeStruct((n, 128), BF16)
+    kv = jax.ShapeDtypeStruct((n, LANES), BF16)
     return pl.pallas_call(
         _qkv_body,
         in_specs=[any_, vm, vm, vm, any_, any_, any_, any_],
         out_specs=[any_] * 6,
         out_shape=[jax.ShapeDtypeStruct((2, 2 * m, qw), BF16), kv, kv, kv, kv, jax.ShapeDtypeStruct(wo.shape, BF16)],
         scratch_shapes=[
-            pltpu.VMEM((4, m // 4, d), BF16),
+            pltpu.VMEM((SP, m // SP, d), BF16),
             pltpu.VMEM((m, d), BF16),
             pltpu.VMEM((2, d, qw), BF16),
-            pltpu.VMEM((2, d, 256), BF16),
-            pltpu.VMEM((4, m, qw), BF16),
-            pltpu.VMEM((4, m, 128), BF16),
-            pltpu.VMEM((4, m, 128), BF16),
-            pltpu.SemaphoreType.DMA((4,)),
+            pltpu.VMEM((2, d, RB), BF16),
+            pltpu.VMEM((SP, m, qw), BF16),
+            pltpu.VMEM((SP, m, LANES), BF16),
+            pltpu.VMEM((SP, m, LANES), BF16),
+            pltpu.SemaphoreType.DMA((SP,)),
             pltpu.SemaphoreType.DMA((2, 3)),
-            pltpu.SemaphoreType.DMA((2, 4, 2, 2)),
-            pltpu.SemaphoreType.DMA((2, 4, 2, 2)),
+            pltpu.SemaphoreType.DMA((2, SP, 2, 2)),
+            pltpu.SemaphoreType.DMA((2, SP, 2, 2)),
             pltpu.SemaphoreType.DMA((2, 2, 2)),
-            pltpu.SemaphoreType.DMA((4, 2)),
+            pltpu.SemaphoreType.DMA((SP, 2)),
             pltpu.SemaphoreType.DMA((2, 2)),
             pltpu.SemaphoreType.DMA((1,)),
             pltpu.SemaphoreType.DMA((1,)),
         ],
-        compiler_params=pltpu.CompilerParams(collective_id=1, has_side_effects=True, vmem_limit_bytes=56 * 2**20),
-        cost_estimate=pl.CostEstimate(flops=2 * m * d * (4 * qw + 1024), bytes_accessed=80 * 2**20, transcendentals=0),
+        compiler_params=pltpu.CompilerParams(collective_id=1, has_side_effects=True, vmem_limit_bytes=KERNEL_VMEM),
+        cost_estimate=pl.CostEstimate(flops=2 * m * d * (SP * qw + 1024), bytes_accessed=80 * MIB, transcendentals=0),
         name="qkv_exchange",
     )(x, g1.reshape(1, -1), cos, sin, wq, wk, wv, wo)
 
@@ -247,10 +256,10 @@
     step = pl.program_id(0)
     order = _sp_order(s)
     far, diag, mate = order[:3]
-    nh = q_ref.shape[2] // 128
+    nh = q_ref.shape[2] // LANES
     m = q_ref.shape[1] * 2
-    xrow = s // 2 * (2 * m)
-    qr = wo_hbm.shape[0] // 4
+    xrow = s // CORES * (2 * m)
+    qr = wo_hbm.shape[0] // SP
     grp, cc, half = _place(step, tp)
     r = 2 * cc + half
     nk = kb.shape[1]
@@ -279,7 +288,7 @@
 
     @pl.when(step == 0)
     def _():
-        for g in range(2):
+        for g in range(CORES):
             for c in kv_copies(g):
                 c.start()
         _barrier([(rep, tp, far), (rep, tp, mate), (rep, 1 - tp, s), (rep, 1 - tp, mate)])
@@ -289,15 +298,15 @@
         wo_x(1).start()
         wo_near(0).start()
         eye[...] = (lax.broadcasted_iota(jnp.int32, eye.shape, 0) == lax.broadcasted_iota(jnp.int32, eye.shape, 1)).astype(F32).astype(BF16)
-        for g in range(2):
+        for g in range(CORES):
             for c in kv_copies(g):
                 c.wait()
 
-            @pl.loop(0, nk // 512)
+            @pl.loop(0, nk // TILE)
             def _(j, g=g):
-                r0 = pl.multiple_of(j * 512, 512)
-                vt[g, :, pl.ds(r0, 512)] = lax.dot_general(
-                    eye[:128, :128], vb[g, pl.ds(r0, 512), :], (((1,), (1,)), ((), ())), preferred_element_type=F32).astype(BF16)
+                r0 = pl.multiple_of(j * TILE, TILE)
+                vt[g, :, pl.ds(r0, TILE)] = lax.dot_general(
+                    eye[:LANES, :LANES], vb[g, pl.ds(r0, TILE), :], (((1,), (1,)), ((), ())), preferred_element_type=F32).astype(BF16)
 
     ms[...] = jnp.full_like(ms, NEG)
     ls[...] = jnp.zeros_like(ls)
@@ -310,7 +319,7 @@
         vv_ = vt[grp, :, pl.ds(k0, n)]
 
         def scores(h):
-            return lax.dot_general(kk_, q_ref[0, :, h * 128:(h + 1) * 128], (((1,), (1,)), ((), ())), preferred_element_type=F32)
+            return lax.dot_general(kk_, q_ref[0, :, h * LANES:(h + 1) * LANES], (((1,), (1,)), ((), ())), preferred_element_type=F32)
 
         sc = scores(0)
         for h in range(nh):
@@ -343,13 +352,13 @@
     blk(start, BQ, True)
     for h in range(nh):
         o = acc[h] * (1.0 / ls[h:h + 1, :])
-        ob[step, :, h * 128:(h + 1) * 128] = lax.dot_general(
+        ob[step, :, h * LANES:(h + 1) * LANES] = lax.dot_general(
             eye[...], o.astype(BF16), (((1,), (1,)), ((), ())), preferred_element_type=F32).astype(BF16)
 
     w = q_ref.shape[2]
 
     def cols(src_s, g):
-        return pl.ds(pl.multiple_of((src_s + 2 * g) % 4 * w, 128), w)
+        return pl.ds(pl.multiple_of((src_s + 2 * g) % SP * w, LANES), w)
 
     def dst(ref, slot, src_s, g):
         return ref.at[slot, :, cols(src_s, g)]
@@ -373,8 +382,8 @@
         cc, nr = _place(t, tp)[1], first_rows(g)
         return pltpu.make_async_remote_copy(
             src_ref=ob.at[t, pl.ds(0, nr), :], dst_ref=oth_hbm.at[pl.ds(0, nr), cols(s, g)],
-            send_sem=ssem.at[1, t], recv_sem=rsem1.at[s % 2, g],
-            device_id=(rep, 1 - tp, s // 2 * 2 + cc), device_id_type=MESH)
+            send_sem=ssem.at[1, t], recv_sem=rsem1.at[s % CORES, g],
+            device_id=(rep, 1 - tp, s // CORES * 2 + cc), device_id_type=MESH)
 
     def to_late2(t):
         cc = _place(t, tp)[1]
@@ -398,7 +407,7 @@
         to_late(step).start()
 
     def mine(t):
-        return _place(t, tp)[1] == s % 2
+        return _place(t, tp)[1] == s % CORES
 
     @pl.when(mine(step))
     def _():
@@ -435,7 +444,7 @@
         wo_x(3).wait_recv()
         wo_near_far(3).start()
 
-        for t in range(4):
+        for t in range(SP):
             to_oth(t, t % 2).wait_send()
             to_late(t + 4).wait()
         to_late2(1).wait()
@@ -451,20 +460,20 @@
             def _():
                 to_own(t).wait_send()
 
-        for g in range(2):
-            for slot in range(2):
+        for g in range(CORES):
+            for slot in range(CORES):
                 pltpu.make_async_remote_copy(
                     src_ref=ob.at[0], dst_ref=dst(own_hbm, slot, mate, g), send_sem=ssem.at[0, 0], recv_sem=rsem0.at[g, slot],
                     device_id=(rep, tp, mate), device_id_type=MESH).wait_recv()
-            for core in range(2):
-                src_s = s // 2 * 2 + core
+            for core in range(CORES):
+                src_s = s // CORES * 2 + core
                 pltpu.make_async_remote_copy(
                     src_ref=ob.at[0, pl.ds(0, first_rows(g)), :], dst_ref=oth_hbm.at[pl.ds(0, first_rows(g)), cols(src_s, g)],
                     send_sem=ssem.at[1, 0], recv_sem=rsem1.at[core, g],
                     device_id=(rep, 1 - tp, src_s), device_id_type=MESH).wait_recv()
         for c in wo_y:
             c.wait_send()
-        for k in range(4):
+        for k in range(SP):
             wo_x(k).wait_send()
         for k in range(3):
             wo_near(k).wait()
@@ -475,24 +484,24 @@
 def _attention(q, k0, v0, k1, v1, wo, wo_oth):
     n = k0.shape[0]
     _, m2, w = q.shape
-    nh = w // 128
+    nh = w // LANES
     steps = 2 * m2 // BQ
     any_ = pl.BlockSpec(memory_space=pl.ANY)
-    shape = jax.ShapeDtypeStruct((2, BQ, 4 * w), BF16)
+    shape = jax.ShapeDtypeStruct((2, BQ, SP * w), BF16)
     return pl.pallas_call(
         _attn_body,
         grid=(steps,),
         in_specs=[pl.BlockSpec((1, BQ, w), lambda t: (t % 2, t // 2, 0))] + [any_] * 6,
         out_specs=[any_] * 5,
-        out_shape=[shape, jax.ShapeDtypeStruct((BQ, 4 * w), BF16), jax.ShapeDtypeStruct(wo.shape, BF16),
+        out_shape=[shape, jax.ShapeDtypeStruct((BQ, SP * w), BF16), jax.ShapeDtypeStruct(wo.shape, BF16),
                    jax.ShapeDtypeStruct((2, 2, BQ, w), BF16), jax.ShapeDtypeStruct((2, LATE_ROWS, w), BF16)],
         input_output_aliases={6: 2},
         scratch_shapes=[
-            pltpu.VMEM((2, n, 128), BF16),
-            pltpu.VMEM((2, n, 128), BF16),
-            pltpu.VMEM((2, 128, n), BF16),
+            pltpu.VMEM((2, n, LANES), BF16),
+            pltpu.VMEM((2, n, LANES), BF16),
+            pltpu.VMEM((2, LANES, n), BF16),
             pltpu.VMEM((BQ, BQ), BF16),
-            pltpu.VMEM((nh, 128, BQ), F32),
+            pltpu.VMEM((nh, LANES, BQ), F32),
             pltpu.VMEM((8, BQ), F32),
             pltpu.VMEM((8, BQ), F32),
             pltpu.VMEM((steps, BQ, w), BF16),
@@ -506,8 +515,8 @@
             pltpu.SemaphoreType.DMA((4, 5)),
             pltpu.SemaphoreType.DMA((4, 5)),
         ],
-        compiler_params=pltpu.CompilerParams(collective_id=2, has_side_effects=True, vmem_limit_bytes=56 * 2**20),
-        cost_estimate=pl.CostEstimate(flops=2 * n * n * w * 2, bytes_accessed=16 * 2**20, transcendentals=0),
+        compiler_params=pltpu.CompilerParams(collective_id=2, has_side_effects=True, vmem_limit_bytes=KERNEL_VMEM),
+        cost_estimate=pl.CostEstimate(flops=2 * n * n * w * 2, bytes_accessed=16 * MIB, transcendentals=0),
         name="attention_exchange",
     )(q, k0, v0, k1, v1, wo, wo_oth)
 
@@ -515,7 +524,7 @@
 NWO, NHID, NW2 = 8, 28, 16
 UNITS = NWO + NHID + NW2
 NBUF = 3
-MB = 256
+MB = RB
 
 
 def _mlp_body(chunks, own_hbm, oth_hbm, x_hbm, wo_hbm, wo_oth_hbm, g_ref, w1_hbm, w3_hbm, w2_hbm, late_hbm, late2_hbm, y_hbm, olate_hbm, olate2_hbm,
@@ -531,15 +540,15 @@
         return pl.ds(pl.multiple_of(j * w, w), w)
 
     def wo_copies(j, sl):
-        return [pltpu.make_async_copy(wo_hbm.at[:, col(j, 512)], wb.at[sl, pl.ds(0, hr), :], wsem.at[sl, 0]),
-                pltpu.make_async_copy(wo_oth_hbm.at[:, col(j, 512)], wb.at[sl, pl.ds(hr, hr), :], wsem.at[sl, 1])]
+        return [pltpu.make_async_copy(wo_hbm.at[:, col(j, TILE)], wb.at[sl, pl.ds(0, hr), :], wsem.at[sl, 0]),
+                pltpu.make_async_copy(wo_oth_hbm.at[:, col(j, TILE)], wb.at[sl, pl.ds(hr, hr), :], wsem.at[sl, 1])]
 
     def hid_copies(j, sl):
-        return [pltpu.make_async_copy(w1_hbm.at[:, col(j, 256)], wb.at[sl, :, pl.ds(0, 256)], wsem.at[sl, 0]),
-                pltpu.make_async_copy(w3_hbm.at[:, col(j, 256)], wb.at[sl, :, pl.ds(256, 256)], wsem.at[sl, 1])]
+        return [pltpu.make_async_copy(w1_hbm.at[:, col(j, RB)], wb.at[sl, :, pl.ds(0, RB)], wsem.at[sl, 0]),
+                pltpu.make_async_copy(w3_hbm.at[:, col(j, RB)], wb.at[sl, :, pl.ds(RB, RB)], wsem.at[sl, 1])]
 
     def w2_copies(t, sl):
-        return [pltpu.make_async_copy(w2_hbm.at[pl.ds(pl.multiple_of(t % 2 * kh, 128), kh), col(t // 2, 512)], wb.at[sl, pl.ds(0, kh), :], wsem.at[sl, 0])]
+        return [pltpu.make_async_copy(w2_hbm.at[pl.ds(pl.multiple_of(t % 2 * kh, LANES), kh), col(t // 2, TILE)], wb.at[sl, pl.ds(0, kh), :], wsem.at[sl, 0])]
 
     def issue(g):
         sl, u = g % NBUF, g % UNITS
@@ -565,7 +574,7 @@
         slot, r0, nr = chunks[c]
         base = hm * ((tp + slot + 1) % 2) + r0
         rs = pl.ds(0, nr)
-        xcopy = pltpu.make_async_copy(x_hbm.at[pl.ds(pl.multiple_of(base, 128), nr), :], xbuf.at[rs, :], asem.at[0])
+        xcopy = pltpu.make_async_copy(x_hbm.at[pl.ds(pl.multiple_of(base, LANES), nr), :], xbuf.at[rs, :], asem.at[0])
         cs = [pltpu.make_async_copy(own_hbm.at[slot, pl.ds(r0, nr), :], abuf.at[rs, pl.ds(0, hr)], asem.at[1])]
         late_at = hm - LATE_ROWS
         if slot == 1:
@@ -574,8 +583,8 @@
             cs.append(pltpu.make_async_copy(oth_hbm.at[pl.ds(r0, nr), :], abuf.at[rs, pl.ds(hr, hr)], asem.at[2]))
         else:
             n0 = late_at - r0
-            c0 = pl.multiple_of(s // 2 * (hr // 2), 128)
-            c1 = pl.multiple_of((1 - s // 2) * (hr // 2), 128)
+            c0 = pl.multiple_of(s // CORES * (hr // 2), LANES)
+            c1 = pl.multiple_of((1 - s // CORES) * (hr // 2), LANES)
             ls = pl.ds(n0, LATE_ROWS)
             cs.append(pltpu.make_async_copy(oth_hbm.at[pl.ds(r0, n0), :], abuf.at[pl.ds(0, n0), pl.ds(hr, hr)], asem.at[2]))
             cs.append(pltpu.make_async_copy(oth_hbm.at[pl.ds(late_at, LATE_ROWS), pl.ds(c0, hr // 2)], abuf.at[ls, pl.ds(hr + c0, hr // 2)], asem.at[3]))
@@ -588,26 +597,26 @@
     xc.start()
     for c in ac:
         c.start()
-    mate = s + 1 - 2 * (s % 2)
+    mate = s + 1 - 2 * (s % CORES)
     _barrier([partner, (rep, 1 - tp, mate)])
     w = late_hbm.shape[3]
 
     def late(g, cc, src_s):
         return pltpu.make_async_remote_copy(
-            src_ref=late_hbm.at[g, cc], dst_ref=olate_hbm.at[:, pl.ds(pl.multiple_of((src_s + 2 * g) % 4 * w, 128), w)],
-            send_sem=lasem.at[g, cc], recv_sem=larsem.at[g, src_s % 2],
-            device_id=(rep, 1 - tp, s // 2 * 2 + cc), device_id_type=MESH)
+            src_ref=late_hbm.at[g, cc], dst_ref=olate_hbm.at[:, pl.ds(pl.multiple_of((src_s + 2 * g) % SP * w, LANES), w)],
+            send_sem=lasem.at[g, cc], recv_sem=larsem.at[g, src_s % CORES],
+            device_id=(rep, 1 - tp, s // CORES * 2 + cc), device_id_type=MESH)
 
     def late2(cc, src_s):
         return pltpu.make_async_remote_copy(
-            src_ref=late2_hbm.at[cc], dst_ref=olate2_hbm.at[:, pl.ds(pl.multiple_of(src_s % 2 * w, 128), w)],
-            send_sem=l2sem.at[cc], recv_sem=l2rsem.at[src_s % 2],
-            device_id=(rep, 1 - tp, s // 2 * 2 + cc), device_id_type=MESH)
-
-    for cc in range(2):
+            src_ref=late2_hbm.at[cc], dst_ref=olate2_hbm.at[:, pl.ds(pl.multiple_of(src_s % CORES * w, LANES), w)],
+            send_sem=l2sem.at[cc], recv_sem=l2rsem.at[src_s % CORES],
+            device_id=(rep, 1 - tp, s // CORES * 2 + cc), device_id_type=MESH)
+
+    for cc in range(CORES):
         late2(cc, s).start()
-    for g in range(2):
-        for cc in range(2):
+    for g in range(CORES):
+        for cc in range(CORES):
             late(g, cc, s).start()
 
     def send(ci, j):
@@ -615,18 +624,18 @@
         return pltpu.make_async_remote_copy(src_ref=pbuf.at[j, pl.ds(r0, nr), :], dst_ref=rbuf.at[j, pl.ds(r0, nr), :],
                                             send_sem=ssem.at[ci, j], recv_sem=rsem.at[ci, j], device_id=partner, device_id_type=MESH)
 
-    yr0 = pl.multiple_of(tp * hm, 128)
+    yr0 = pl.multiple_of(tp * hm, LANES)
 
     def ysend(j):
-        return pltpu.make_async_remote_copy(src_ref=ybuf.at[j], dst_ref=y_hbm.at[pl.ds(yr0, hm), col(j, 512)],
+        return pltpu.make_async_remote_copy(src_ref=ybuf.at[j], dst_ref=y_hbm.at[pl.ds(yr0, hm), col(j, TILE)],
                                             send_sem=ysem.at[j], recv_sem=yrsem.at[j], device_id=partner, device_id_type=MESH)
 
     def yrecv(j):
-        return pltpu.make_async_remote_copy(src_ref=ybuf.at[j], dst_ref=y_hbm.at[pl.ds(pl.multiple_of((1 - tp) * hm, 128), hm), col(j, 512)],
+        return pltpu.make_async_remote_copy(src_ref=ybuf.at[j], dst_ref=y_hbm.at[pl.ds(pl.multiple_of((1 - tp) * hm, LANES), hm), col(j, TILE)],
                                             send_sem=ysem.at[j], recv_sem=yrsem.at[j], device_id=partner, device_id_type=MESH)
 
     def yown(j):
-        return pltpu.make_async_copy(ybuf.at[j], y_hbm.at[pl.ds(yr0, hm), col(j, 512)], ylsem.at[j])
+        return pltpu.make_async_copy(ybuf.at[j], y_hbm.at[pl.ds(yr0, hm), col(j, TILE)], ylsem.at[j])
 
     nsend = len(chunks) - 1
     for ci, (slot, r0, nr) in enumerate(chunks):
@@ -646,11 +655,11 @@
             for b in range(nr // MB):
                 rs = pl.ds(b * MB, MB)
                 o = jnp.dot(abuf[rs, :], wb[sl], preferred_element_type=F32)
-                xbuf[rs, col(j, 512)] = (xbuf[rs, col(j, 512)].astype(F32) + o).astype(BF16)
-
-        @pl.loop(0, nr // 64)
+                xbuf[rs, col(j, TILE)] = (xbuf[rs, col(j, TILE)].astype(F32) + o).astype(BF16)
+
+        @pl.loop(0, nr // HALF)
         def _(i):
-            rs = pl.ds(pl.multiple_of(i * 64, 64), 64)
+            rs = pl.ds(pl.multiple_of(i * HALF, HALF), HALF)
             xs = xbuf[rs, :].astype(F32)
             r = lax.rsqrt(jnp.mean(xs * xs, axis=-1, keepdims=True) + EPS)
             abuf[rs, :] = (xs * r * g_ref[...]).astype(BF16)
@@ -668,16 +677,16 @@
             for b in range(nr // MB):
                 rs = pl.ds(b * MB, MB)
                 ab = jnp.dot(abuf[rs, :], wb[sl], preferred_element_type=F32)
-                a = ab[:, :256]
-                hid[rs, col(j, 256)] = (a / (1.0 + jnp.exp(-a)) * ab[:, 256:]).astype(BF16)
+                a = ab[:, :RB]
+                hid[rs, col(j, RB)] = (a / (1.0 + jnp.exp(-a)) * ab[:, RB:]).astype(BF16)
 
         if ci + 3 == len(chunks):
-            for core in range(2):
-                late2(core, s // 2 * 2 + core).wait_recv()
+            for core in range(CORES):
+                late2(core, s // CORES * 2 + core).wait_recv()
         if ci + 2 == len(chunks):
-            for g in range(2):
-                for core in range(2):
-                    late(g, core, s // 2 * 2 + core).wait_recv()
+            for g in range(CORES):
+                for core in range(CORES):
+                    late(g, core, s // CORES * 2 + core).wait_recv()
         if ci + 1 < len(chunks):
             for c in acts(ci + 1)[1]:
                 c.start()
@@ -685,7 +694,7 @@
         @pl.loop(0, NW2 // 2)
         def _(j, g0=g0, ci=ci, slot=slot, r0=r0, nr=nr):
             g = g0 + NWO + NHID + 2 * j
-            for h in range(2):
+            for h in range(CORES):
                 sl = (g + h) % NBUF
                 issue(g + h + NBUF - 1)
                 for c in w2_copies(2 * j + h, sl):
@@ -703,16 +712,16 @@
                             for k in range(nsend):
                                 send(k, j).wait_recv()
                         o = o + pbuf[NW2 // 2, ps, :] + rbuf[j, ps, :]
-                        ybuf[j, ps, :] = (xbuf[rs, col(j, 512)].astype(F32) + o).astype(BF16)
+                        ybuf[j, ps, :] = (xbuf[rs, col(j, TILE)].astype(F32) + o).astype(BF16)
             if slot == 0:
                 send(ci, j).start()
             else:
                 ysend(j).start()
                 yown(j).start()
 
-    for cc in range(2):
+    for cc in range(CORES):
         late2(cc, s).wait_send()
-        for g in range(2):
+        for g in range(CORES):
             late(g, cc, s).wait_send()
 
     @pl.loop(0, NW2 // 2)
@@ -727,7 +736,7 @@
 def _mlp(own, oth, late, late2, x, wo, wo_oth, g2, w1, w3, w2):
     m, d = x.shape
     hm = m // 2
-    chunks = ((0, 0, 256), (0, 256, 256), (1, 0, 512))
+    chunks = ((0, 0, RB), (0, RB, RB), (1, 0, TILE))
     any_ = pl.BlockSpec(memory_space=pl.ANY)
     vm = pl.BlockSpec(memory_space=pltpu.VMEM)
     nt = NW2 // 2
@@ -738,13 +747,13 @@
         out_shape=[jax.ShapeDtypeStruct((m, d), BF16), jax.ShapeDtypeStruct((hm, wo.shape[0]), BF16),
                    jax.ShapeDtypeStruct((LATE_ROWS, wo.shape[0] // 2), BF16)],
         scratch_shapes=[
-            pltpu.VMEM((NBUF, d, 512), BF16),
+            pltpu.VMEM((NBUF, d, TILE), BF16),
             pltpu.VMEM((hm, d), BF16),
             pltpu.VMEM((hm, d), BF16),
             pltpu.VMEM((hm, w2.shape[0]), BF16),
-            pltpu.VMEM((nt + 1, hm, 512), F32),
-            pltpu.VMEM((nt, hm, 512), F32),
-            pltpu.VMEM((nt, hm, 512), BF16),
+            pltpu.VMEM((nt + 1, hm, TILE), F32),
+            pltpu.VMEM((nt, hm, TILE), F32),
+            pltpu.VMEM((nt, hm, TILE), BF16),
             pltpu.SemaphoreType.DMA((NBUF, 2)),
             pltpu.SemaphoreType.DMA((5,)),
             pltpu.SemaphoreType.DMA((2, nt)),
@@ -757,8 +766,8 @@
             pltpu.SemaphoreType.DMA((2,)),
             pltpu.SemaphoreType.DMA((2,)),
         ],
-        compiler_params=pltpu.CompilerParams(collective_id=3, has_side_effects=True, vmem_limit_bytes=67043328),
-        cost_estimate=pl.CostEstimate(flops=2 * m * d * (d + 3 * w1.shape[1]), bytes_accessed=640 * 2**20, transcendentals=0),
+        compiler_params=pltpu.CompilerParams(collective_id=3, has_side_effects=True, vmem_limit_bytes=MAX_VMEM),
+        cost_estimate=pl.CostEstimate(flops=2 * m * d * (d + 3 * w1.shape[1]), bytes_accessed=640 * MIB, transcendentals=0),
         name="mlp_sum",
     )(own, oth, x, wo, wo_oth, g2.reshape(1, -1), w1, w3, w2, late, late2)[0]
 
@@ -788,7 +797,7 @@
         out_specs=[any_] * 3,
         out_shape=[jax.ShapeDtypeStruct(a.shape, a.dtype) for a in arrays],
         scratch_shapes=[pltpu.VMEM((8, m // 8, d), BF16), pltpu.VMEM((2, *k.shape), BF16), pltpu.SemaphoreType.DMA((2, 10))],
-        compiler_params=pltpu.CompilerParams(vmem_limit_bytes=67043328),
+        compiler_params=pltpu.CompilerParams(vmem_limit_bytes=MAX_VMEM),
         name="result_copy",
     )(*arrays)
 
@@ -807,7 +816,7 @@
         own, oth, wo_oth, late, late2 = _attention(q, k, v, k1, v1, wo, wo_oth)
         y = _mlp(own, oth, late, late2, x, wo, wo_oth, g2, w1, w3, w2)
         y, k, v = _copy(y, k, v)
-        return y, k.reshape(n, 1, 128), v.reshape(n, 1, 128)
+        return y, k.reshape(n, 1, LANES), v.reshape(n, 1, LANES)
 
     return jax.shard_map(
         local,

time: 489 us -> 489 us (level)
  no operation moved by 1% of the time
where the time goes in v5:
time: 489 us; the launch traced here: 488 us
  Pallas kernels  483 us (99%)
    pallas_call x1, Pallas kernels, _mlp(): pl.pallas_call(functools.partial(_mlp_body, chunks), in_specs=[any_] * 5...  327 us
    pallas_call x1, Pallas kernels, _attention(): pl.pallas_call(_attn_body, grid=(steps,), in_specs=[pl.BlockSpec((1, BQ,...  92.3 us
    pallas_call x1, Pallas kernels, _qkv(): pl.pallas_call(_qkv_body, in_specs=[any_, vm, vm, vm, any_, any_, any_, a...  55.7 us

profile of v5, /device:TPU:0, one launch (start us, length us, event | category | flops | bytes accessed | tf_op | source)
XLA Modules:
  0.0 488.0 jit_solution(17207387790214180861)
XLA Ops:
  0.6 0.7 convert_element_type.10
  1.3 3.0 fusion
  4.4 55.7 %qkv_exchange.1 = (bf16[2,2048,512]{2,1,0:T(8,128)(2,1)}, bf16[4096,128]{1,0:T(8,128)(2,1)}, bf16[4096,128]{1,0:T(8,128)(2,1)}, bf16[4096,128]{1,0:T(8,128)(2,1)...) custom-call(bf16[1024,4096]{1,0:T(8,128)(2,1)} %x_hbm.3, f32[1,4096]{1,0:T(1,128)} %bitcast.6, ...), custom_call_target="tpu_custom_call" | custom-call | flops 25769803776 | bytes 83886080 | tf_op jit(solution)/shard_map/qkv_exchange/pallas_call | solution.py:219
  60.0 92.3 %attention_exchange.1 = (bf16[2,512,2048]{2,1,0:T(8,128)(2,1)}, bf16[512,2048]{1,0:T(8,128)(2,1)}, bf16[2048,4096]{1,0:T(8,128)(2,1)}, bf16[2,2,512,512]{3,2,1,0:T(8,128)(2,1)}, bf16[2,128,512]{2,1,0:T(8,128)(2,1)}) custom-call(bf16[2,2048,512]{2,1,0:T(8,128)(2,1)} %get-tuple-element.18.q_ref, ...), custom_call_target="tpu_custom_call", output_to_operand_aliasing={{2}: (6, {})} | custom-call | flops 34359738368 | bytes 16777216 | tf_op jit(solution)/shard_map/attention_exchange/pallas_call | solution.py:491
  152.3 327.3 %mlp_sum.1 = (bf16[1024,4096]{1,0:T(8,128)(2,1)}, bf16[512,2048]{1,0:T(8,128)(2,1)}, bf16[128,1024]{1,0:T(8,128)(2,1)}) custom-call(bf16[2,512,2048]{2,1,0:T(8,128)(2,1)} %get-tuple-element.24.own_hbm, bf16[512,2048]{1,0:T(8,128)(2,1)} %get-tuple-element.25.oth_hbm, bf16[1024,4096]{1,0:T(8,128)(2,1)} %x_hbm.3, bf16[2048,4096]{1,0:T(8,128)(2,1)} %wo_hbm.5, ...), custom_call_target="tpu_custom_call" | custom-call | flops 214748364800 | bytes 671088640 | tf_op jit(solution)/shard_map/mlp_sum/pallas_call | solution.py:743
  479.6 8.2 %result_copy.1 = (bf16[1024,4096]{1,0:T(8,128)(2,1)}, bf16[4096,128]{1,0:T(8,128)(2,1)}, bf16[4096,128]{1,0:T(8,128)(2,1)}) custom-call(bf16[1024,4096]{1,0:T(8,128)(2,1)} %get-tuple-element.29.y_ref, bf16[4096,128]{1,0:T(8,128)(2,1)} %get-tuple-element.19.k0_hbm.k_ref, bf16[4096,128]{1,0:T(8,128)(2,1)} %get-tuple-element.20.v0_hbm.v_ref), custom_call_target="tpu_custom_call" | custom-call | tf_op jit(solution)/shard_map/result_copy/pallas_call | solution.py:794
  (1 shorter events, 0.0 us)

commit v6 on v5

--- a/solution.py
+++ b/solution.py
@@ -774,8 +774,8 @@
 
 def _copy_body(y_ref, k_ref, v_ref, yo_ref, ko_ref, vo_ref, buf, kbuf, sem):
     n, nr = buf.shape[:2]
-    moves = [(y_ref.at[pl.ds(i * nr, nr), :], yo_ref.at[pl.ds(i * nr, nr), :], buf.at[i]) for i in range(n)]
-    moves += [(k_ref, ko_ref, kbuf.at[0]), (v_ref, vo_ref, kbuf.at[1])]
+    moves = [(k_ref, ko_ref, kbuf.at[0]), (v_ref, vo_ref, kbuf.at[1])]
+    moves += [(y_ref.at[pl.ds(i * nr, nr), :], yo_ref.at[pl.ds(i * nr, nr), :], buf.at[i]) for i in range(n)]
     get = [pltpu.make_async_copy(a, b, sem.at[0, i]) for i, (a, _, b) in enumerate(moves)]
     put = [pltpu.make_async_copy(b, c, sem.at[1, i]) for i, (_, c, b) in enumerate(moves)]
     for c in get:
@@ -796,7 +796,7 @@
         in_specs=[any_] * 3,
         out_specs=[any_] * 3,
         out_shape=[jax.ShapeDtypeStruct(a.shape, a.dtype) for a in arrays],
-        scratch_shapes=[pltpu.VMEM((8, m // 8, d), BF16), pltpu.VMEM((2, *k.shape), BF16), pltpu.SemaphoreType.DMA((2, 10))],
+        scratch_shapes=[pltpu.VMEM((16, m // 16, d), BF16), pltpu.VMEM((2, *k.shape), BF16), pltpu.SemaphoreType.DMA((2, 18))],
         compiler_params=pltpu.CompilerParams(vmem_limit_bytes=MAX_VMEM),
         name="result_copy",
     )(*arrays)

time: 489 us -> 489 us (level)
  no operation moved by 1% of the time
where the time goes in v6:
time: 489 us; the launch traced here: 488 us
  Pallas kernels  483 us (99%)
    pallas_call x1, Pallas kernels, _mlp(): pl.pallas_call(functools.partial(_mlp_body, chunks), in_specs=[any_] * 5...  327 us
    pallas_call x1, Pallas kernels, _attention(): pl.pallas_call(_attn_body, grid=(steps,), in_specs=[pl.BlockSpec((1, BQ,...  92.3 us
    pallas_call x1, Pallas kernels, _qkv(): pl.pallas_call(_qkv_body, in_specs=[any_, vm, vm, vm, any_, any_, any_, a...  55.7 us

profile of v6, /device:TPU:0, one launch (start us, length us, event | category | flops | bytes accessed | tf_op | source)
XLA Modules:
  0.0 488.0 jit_solution(18090682395677790716)
XLA Ops:
  0.6 0.7 convert_element_type.10
  1.3 3.0 fusion
  4.4 55.7 %qkv_exchange.1 = (bf16[2,2048,512]{2,1,0:T(8,128)(2,1)}, bf16[4096,128]{1,0:T(8,128)(2,1)}, bf16[4096,128]{1,0:T(8,128)(2,1)}, bf16[4096,128]{1,0:T(8,128)(2,1)...) custom-call(bf16[1024,4096]{1,0:T(8,128)(2,1)} %x_hbm.3, f32[1,4096]{1,0:T(1,128)} %bitcast.6, ...), custom_call_target="tpu_custom_call" | custom-call | flops 25769803776 | bytes 83886080 | tf_op jit(solution)/shard_map/qkv_exchange/pallas_call | solution.py:219
  60.0 92.3 %attention_exchange.1 = (bf16[2,512,2048]{2,1,0:T(8,128)(2,1)}, bf16[512,2048]{1,0:T(8,128)(2,1)}, bf16[2048,4096]{1,0:T(8,128)(2,1)}, bf16[2,2,512,512]{3,2,1,0:T(8,128)(2,1)}, bf16[2,128,512]{2,1,0:T(8,128)(2,1)}) custom-call(bf16[2,2048,512]{2,1,0:T(8,128)(2,1)} %get-tuple-element.18.q_ref, ...), custom_call_target="tpu_custom_call", output_to_operand_aliasing={{2}: (6, {})} | custom-call | flops 34359738368 | bytes 16777216 | tf_op jit(solution)/shard_map/attention_exchange/pallas_call | solution.py:491
  152.3 327.3 %mlp_sum.1 = (bf16[1024,4096]{1,0:T(8,128)(2,1)}, bf16[512,2048]{1,0:T(8,128)(2,1)}, bf16[128,1024]{1,0:T(8,128)(2,1)}) custom-call(bf16[2,512,2048]{2,1,0:T(8,128)(2,1)} %get-tuple-element.24.own_hbm, bf16[512,2048]{1,0:T(8,128)(2,1)} %get-tuple-element.25.oth_hbm, bf16[1024,4096]{1,0:T(8,128)(2,1)} %x_hbm.3, bf16[2048,4096]{1,0:T(8,128)(2,1)} %wo_hbm.5, ...), custom_call_target="tpu_custom_call" | custom-call | flops 214748364800 | bytes 671088640 | tf_op jit(solution)/shard_map/mlp_sum/pallas_call | solution.py:743
  479.6 8.2 %result_copy.1 = (bf16[1024,4096]{1,0:T(8,128)(2,1)}, bf16[4096,128]{1,0:T(8,128)(2,1)}, bf16[4096,128]{1,0:T(8,128)(2,1)}) custom-call(bf16[1024,4096]{1,0:T(8,128)(2,1)} %get-tuple-element.29.y_ref, bf16[4096,128]{1,0:T(8,128)(2,1)} %get-tuple-element.19.k0_hbm.k_ref, bf16[4096,128]{1,0:T(8,128)(2,1)} %get-tuple-element.20.v0_hbm.v_ref), custom_call_target="tpu_custom_call" | custom-call | tf_op jit(solution)/shard_map/result_copy/pallas_call | solution.py:794
  (1 shorter events, 0.0 us)
